TPU v7x, 256 devices: a whole 4x4x8 slice. The times are simulated.
256 devices in a mesh: member: 8 (over y_lo, x), grid: 32 (over z, y_hi, core).
Axes of the slice: x: 4, y: 4 (y_hi: 2, y_lo: 2; y = y_hi * 2 + y_lo), z: 8, core: 2. Of those that a mesh axis runs over, the one named last changes fastest.
Arguments:
- prior_ensemble: bfloat16 [40, 48, 131072], P('member', None, 'grid'), may hold values from -6 to 6
- domain_site_mapping: int32 [32, 8, 512], P(None, None, 'grid'), may hold values from 0 to 4095, as said below
- neighbour_triples: int32 [32, 3, 4096], P('grid', None, 'member'), may hold values from 0 to 159
- stencil_factors: float32 [32, 3, 4096], P('grid', None, 'member'), may hold values from 0.1 to 1
- sparse_node_transforms: float32 [1600, 4096], P(None, 'grid'), may hold values from -0.4 to 1.8
Outputs:
- analysis: bfloat16 [40, 48, 131072], P('member', None, 'grid')
Inputs may be any that keep to these rules, and one draw needn't show every extreme that they name: For every model patch h, the entries domain_site_mapping[:, :, h * 16 : (h + 1) * 16] hold every number from 0 to 4095 exactly once.
All inputs are finite; a program needn't handle non-finite values.
Results may differ from a plain program's by a relative error of at most 0.0076.
Values may be sent and summed in bfloat16 or wider, within the bound.
No kernel may reach another device: no remote copies, remote signals or barrier semaphores. Data moves between devices by JAX's collectives and lax.ppermute only.
A program may use at most 128 MiB of HBM per device.

v0:
```python
import jax
import jax.numpy as jnp
from jax import lax
from jax.experimental import pallas as pl
from jax.experimental.pallas import tpu as pltpu
from jax.sharding import PartitionSpec as P

ENSEMBLE_SIZE = 40
RIM = 16
VMEM_LIMIT = 48 * 1024 * 1024


def full_spec(shape):
    return pl.BlockSpec(shape, lambda *_: (0,) * len(shape))


def pick_kernel(rows_ref, targets_ref, out_ref):
    cells = rows_ref.shape[1]
    columns = targets_ref.shape[2]
    cell_ids = lax.broadcasted_iota(jnp.int32, (cells, columns), 0)
    onehot = jnp.where(cell_ids == targets_ref[0], 1.0, 0.0).astype(jnp.bfloat16)
    out_ref[0] = jnp.dot(rows_ref[...], onehot, preferred_element_type=jnp.float32).astype(
        jnp.bfloat16
    )


def pick_columns(source_rows, targets):
    rows, cells = source_rows.shape
    groups, _, columns = targets.shape
    return pl.pallas_call(
        pick_kernel,
        grid=(groups,),
        in_specs=[
            full_spec((rows, cells)),
            pl.BlockSpec((1, 1, columns), lambda i: (i, 0, 0)),
        ],
        out_specs=pl.BlockSpec((1, rows, columns), lambda i: (i, 0, 0)),
        out_shape=jax.ShapeDtypeStruct((groups, rows, columns), jnp.bfloat16),
        compiler_params=pltpu.CompilerParams(vmem_limit_bytes=VMEM_LIMIT),
        name="pick",
    )(source_rows, targets)


def place_kernel(parts_ref, positions_ref, out_ref, rows_ref):
    groups, _, columns = parts_ref.shape
    block = out_ref.shape[1]
    step = pl.program_id(0)

    @pl.when(step == 0)
    def _():
        for group in range(groups):
            rows_ref[:, group * columns : (group + 1) * columns] = parts_ref[group]

    positions = positions_ref[...]
    lanes = positions.shape[1]
    wide = jnp.concatenate([positions] * (block // lanes), axis=1)
    target_ids = step * block + lax.broadcasted_iota(jnp.int32, (groups * columns, block), 1)
    onehot = jnp.where(wide == target_ids, 1.0, 0.0).astype(jnp.bfloat16)
    out_ref[...] = jnp.dot(
        rows_ref[...], onehot, preferred_element_type=jnp.float32
    ).astype(jnp.bfloat16)


def place_columns(parts, positions):
    groups, rows, columns = parts.shape
    cells = groups * columns
    return pl.pallas_call(
        place_kernel,
        grid=(groups,),
        in_specs=[full_spec(parts.shape), full_spec(positions.shape)],
        out_specs=pl.BlockSpec((rows, columns), lambda i: (0, i)),
        out_shape=jax.ShapeDtypeStruct((rows, cells), jnp.bfloat16),
        scratch_shapes=[pltpu.VMEM((rows, cells), jnp.bfloat16)],
        compiler_params=pltpu.CompilerParams(vmem_limit_bytes=VMEM_LIMIT),
        name="place",
    )(parts, positions)


def turn_kernel(transforms_ref, out_ref):
    out_ref[...] = jnp.transpose(transforms_ref[...]).astype(jnp.bfloat16)


def turn(transforms):
    entries, points = transforms.shape
    return pl.pallas_call(
        turn_kernel,
        out_shape=jax.ShapeDtypeStruct((points, entries), jnp.bfloat16),
        compiler_params=pltpu.CompilerParams(vmem_limit_bytes=VMEM_LIMIT),
        name="turn",
    )(transforms)


def blend_kernel(left_ref, own_ref, right_ref, points_ref, factors_ref, out_ref):
    rim, points_own = left_ref.shape[0], own_ref.shape[0]
    columns = points_ref.shape[2]
    extent = points_own + 2 * rim
    factors = factors_ref[0]
    shares = factors / jnp.sum(factors, axis=0, keepdims=True)
    slot_ids = lax.broadcasted_iota(jnp.int32, (extent, columns), 0)
    spread = jnp.zeros((extent, columns), jnp.float32)
    for which in range(3):
        spread = spread + jnp.where(
            points_ref[0, which : which + 1, :] == slot_ids, shares[which : which + 1, :], 0.0
        )
    high = spread.astype(jnp.bfloat16)
    low = (spread - high.astype(jnp.float32)).astype(jnp.bfloat16)
    widened = jnp.concatenate([left_ref[...], own_ref[...], right_ref[...]], axis=0)
    dims = (((0,), (0,)), ((), ()))
    out_ref[...] = lax.dot_general(
        jnp.concatenate([high, low], axis=0),
        jnp.concatenate([widened, widened], axis=0),
        dims,
        preferred_element_type=jnp.float32,
    ).astype(jnp.bfloat16)


def blend(left, own, right, points, factors):
    return pl.pallas_call(
        blend_kernel,
        out_shape=jax.ShapeDtypeStruct((points.shape[2], own.shape[1]), jnp.bfloat16),
        compiler_params=pltpu.CompilerParams(vmem_limit_bytes=VMEM_LIMIT),
        name="blend",
    )(left, own, right, points, factors)


def update_kernel(fields_ref, weights_ref, out_ref, turned_ref, deviation_ref, mean_ref):
    members, fields, lanes = fields_ref.shape
    turned_ref[...] = jnp.transpose(weights_ref[...].astype(jnp.float32))
    total = fields_ref[0].astype(jnp.float32)
    for k in range(1, members):
        total = total + fields_ref[k].astype(jnp.float32)
    mean = total * (1.0 / members)
    mean_ref[...] = mean
    for k in range(members):
        deviation = (fields_ref[k].astype(jnp.float32) - mean).astype(jnp.bfloat16)
        deviation_ref[k] = deviation.astype(jnp.float32)
    together = 4

    def body(step, carry):
        base = step * together
        sums = [mean_ref[...] for _ in range(together)]
        for k in range(members):
            deviation = deviation_ref[k]
            for t in range(together):
                weight = turned_ref[pl.ds(k * members + base + t, 1), :]
                sums[t] = sums[t] + deviation * weight
        for t in range(together):
            out_ref[base + t] = sums[t].astype(jnp.bfloat16)
        return carry

    lax.fori_loop(0, members // together, body, 0)


def update(fields, weights):
    members, quantities, columns = fields.shape
    lanes = 128
    return pl.pallas_call(
        update_kernel,
        grid=(columns // lanes,),
        in_specs=[
            pl.BlockSpec((members, quantities, lanes), lambda i: (0, 0, i)),
            pl.BlockSpec((lanes, members * members), lambda i: (i, 0)),
        ],
        out_specs=pl.BlockSpec((members, quantities, lanes), lambda i: (0, 0, i)),
        out_shape=jax.ShapeDtypeStruct(fields.shape, jnp.bfloat16),
        scratch_shapes=[
            pltpu.VMEM((members * members, lanes), jnp.float32),
            pltpu.VMEM((members, quantities, lanes), jnp.float32),
            pltpu.VMEM((quantities, lanes), jnp.float32),
        ],
        compiler_params=pltpu.CompilerParams(vmem_limit_bytes=VMEM_LIMIT),
        name="update",
    )(fields, weights)


def on_device(
    prior_ensemble, domain_site_mapping, neighbour_triples, stencil_factors, sparse_node_transforms
):
    own_members, quantities, cells = prior_ensemble.shape
    groups = lax.axis_size("member")
    patches = lax.axis_size("grid")
    columns = cells // groups
    per_source = columns // patches
    entries = ENSEMBLE_SIZE * ENSEMBLE_SIZE

    turned = turn(sparse_node_transforms)
    following = [(i, (i + 1) % patches) for i in range(patches)]
    preceding = [((i + 1) % patches, i) for i in range(patches)]
    left = lax.ppermute(turned[-RIM:], "grid", following)
    right = lax.ppermute(turned[:RIM], "grid", preceding)

    order = jnp.transpose(domain_site_mapping, (1, 0, 2)).reshape(groups, 1, columns)
    source_rows = prior_ensemble.reshape(own_members * quantities, cells)
    chosen = pick_columns(source_rows, order)
    blended = blend(left, turned, right, neighbour_triples, stencil_factors)
    weights = lax.all_to_all(
        blended.reshape(patches, per_source, entries), "grid", split_axis=0, concat_axis=0, tiled=True
    ).reshape(columns, entries)
    gathered = lax.all_to_all(chosen, "member", split_axis=0, concat_axis=0, tiled=True)
    result = update(gathered.reshape(ENSEMBLE_SIZE, quantities, columns), weights)
    returned = lax.all_to_all(
        result.reshape(groups, own_members * quantities, columns),
        "member",
        split_axis=0,
        concat_axis=0,
        tiled=True,
    )
    positions = jnp.broadcast_to(order.reshape(cells, 1), (cells, 128))
    placed = place_columns(returned, positions)
    return placed.reshape(own_members, quantities, cells)


def solution(mesh):
    return jax.shard_map(
        on_device,
        mesh=mesh,
        in_specs=(
            P("member", None, "grid"),
            P(None, None, "grid"),
            P("grid", None, "member"),
            P("grid", None, "member"),
            P(None, "grid"),
        ),
        out_specs=P("member", None, "grid"),
        check_vma=False,
    )
```

profile of v0, /device:TPU:30, one launch (start us, length us, event | category | flops | bytes accessed | tf_op | source)
XLA Modules:
  0.0 157.0 jit_solution(4850167763992229693)
XLA Ops:
  0.0 0.9 copy.9
  0.9 0.1 reshape.29.targets_ref
  1.1 0.0 copy-start.2
  1.1 1.5 copy-done.2
  2.6 10.5 %pick.1 = bf16[8,240,512]{2,1,0:T(8,128)(2,1)} custom-call(bf16[240,4096]{1,0:T(8,128)(2,1)S(1)} %bitcast.11, s32[8,1,512]{2,1,0:T(1,128)S(1)} %reshape.29.targets_ref), custom_call_target="tpu_custom_call" | custom-call | tf_op jit(solution)/shard_map/pick/pallas_call | solution.py:30
  13.1 0.0 copy-start.3
  13.2 0.0 copy-start.4
  13.2 0.0 copy-start.5
  13.2 5.8 %all-to-all-start = ((bf16[8,240,512]{2,1,0:T(8,128)(2,1)}), bf16[8,240,512]{2,1,0:T(8,128)(2,1)S(1)}, u32[]{:S(2)}, u32[]{:S(2)}) async-start(bf16[8,240,512]{2,1,0:T(8,128)(2,1)} %pick.1), calls=%async_computation | async-start | bytes 3932160 | tf_op jit(solution)/shard_map/all_to_all | solution.py:199
  19.0 0.0 copy-done.3
  19.0 0.2 turn.1.own_ref
  19.2 0.2 collective-permute-start.1
  19.4 0.4 collective-permute-start
  19.8 0.0 copy-done.4
  19.8 0.0 copy-done.5
  19.8 21.2 %collective-permute-done.1.right_ref = bf16[16,1600]{1,0:T(8,128)(2,1)S(1)} collective-permute-done((bf16[16,1600]{1,0:T(8,128)(2,1)S(1)}, bf16[16,1600]{1,0:T(8,128)(2,1)S(1)}, u32[]{:S(2)}, u32[]{:S(2)}) %collective-permute-start.1) | collective-permute-done | bytes 51232 | tf_op jit(solution)/shard_map/ppermute | solution.py:190
  41.0 1.7 %collective-permute-done.left_ref = bf16[16,1600]{1,0:T(8,128)(2,1)S(1)} collective-permute-done((bf16[16,1600]{1,0:T(8,128)(2,1)S(1)}, bf16[16,1600]{1,0:T(8,128)(2,1)S(1)}, u32[]{:S(2)}, u32[]{:S(2)}) %collective-permute-start) | collective-permute-done | bytes 51232 | tf_op jit(solution)/shard_map/ppermute | solution.py:189
  42.7 1.2 blend.1
  43.9 0.0 copy-start.1
  43.9 1.2 copy-done.1
  45.1 0.0 all-to-all-done
  45.1 54.5 %all_to_all.15 = bf16[32,16,1600]{2,1,0:T(8,128)(2,1)S(1)} all-to-all(bf16[32,16,1600]{2,1,0:T(8,128)(2,1)} %bitcast.9), channel_id=1, replica_groups=mesh['member'=8,'grid'=32] {'grid'}, dimensions={0} | all-to-all | bytes 3276800 | tf_op jit(solution)/shard_map/all_to_all | solution.py:196
  99.7 14.4 %update.1 = bf16[40,48,512]{2,1,0:T(8,128)(2,1)S(1)} custom-call(bf16[40,48,512]{2,1,0:T(8,128)(2,1)S(1)} %bitcast.7, bf16[512,1600]{1,0:T(8,128)(2,1)S(1)} %bitcast.10), custom_call_target="tpu_custom_call" | custom-call | tf_op jit(solution)/shard_map/update/pallas_call | solution.py:157
  114.1 0.0 copy-start
  114.1 1.3 copy-done
  115.4 5.7 %all-to-all-start.2 = ((bf16[8,240,512]{2,1,0:T(8,128)(2,1)}), bf16[8,240,512]{2,1,0:T(8,128)(2,1)S(1)}, u32[]{:S(2)}, u32[]{:S(2)}) async-start(bf16[8,240,512]{2,1,0:T(8,128)(2,1)} %bitcast.8), calls=%async_computation.2 | async-start | bytes 3932160 | tf_op jit(solution)/shard_map/all_to_all | solution.py:201
  121.1 0.1 broadcast_in_dim.7
  121.2 24.8 %all-to-all-done.2.parts_ref = bf16[8,240,512]{2,1,0:T(8,128)(2,1)S(1)} async-done(((bf16[8,240,512]{2,1,0:T(8,128)(2,1)}), bf16[8,240,512]{2,1,0:T(8,128)(2,1)S(1)}, u32[]{:S(2)}, u32[]{:S(2)}) %all-to-all-start.2) | async-done | bytes 1966112 | tf_op jit(solution)/shard_map/all_to_all | solution.py:201
  145.9 0.6 broadcast_in_dim.8.positions_ref
  146.5 10.4 %place.1 = bf16[240,4096]{1,0:T(8,128)(2,1)} custom-call(bf16[8,240,512]{2,1,0:T(8,128)(2,1)S(1)} %all-to-all-done.2.parts_ref, s32[4096,128]{1,0:T(8,128)S(1)} %broadcast_in_dim.8.positions_ref), custom_call_target="tpu_custom_call" | custom-call | tf_op jit(solution)/shard_map/place/pallas_call | solution.py:67
  (3 shorter events, 0.0 us)
Async XLA Ops:
  1.1 1.5 copy-start.2
  13.1 5.8 %copy-start.3 = (f32[1600,128]{1,0:T(8,128)S(1)}, f32[1600,128]{1,0:T(8,128)}, u32[]{:S(2)}) copy-start(f32[1600,128]{1,0:T(8,128)} %transforms_ref.1) | copy-start | bytes 2457604
  13.2 6.6 %copy-start.4 = (s32[1,3,512]{2,0,1:T(1,128)S(1)}, s32[1,3,512]{2,0,1:T(1,128)}, u32[]{:S(2)}) copy-start(s32[1,3,512]{2,0,1:T(1,128)} %param.7) | copy-start | bytes 18436
  13.2 6.6 %copy-start.5 = (f32[1,3,512]{2,0,1:T(1,128)S(1)}, f32[1,3,512]{2,0,1:T(1,128)}, u32[]{:S(2)}) copy-start(f32[1,3,512]{2,0,1:T(1,128)} %param.8) | copy-start | bytes 18436
  13.2 32.0 %all-to-all-start = ((bf16[8,240,512]{2,1,0:T(8,128)(2,1)}), bf16[8,240,512]{2,1,0:T(8,128)(2,1)S(1)}, u32[]{:S(2)}, u32[]{:S(2)}) async-start(bf16[8,240,512]{2,1,0:T(8,128)(2,1)} %pick.1), calls=%async_computation | async-start | bytes 3932160 | tf_op jit(solution)/shard_map/all_to_all | solution.py:199
  19.2 21.9 %collective-permute-start.1 = (bf16[16,1600]{1,0:T(8,128)(2,1)S(1)}, bf16[16,1600]{1,0:T(8,128)(2,1)S(1)}, u32[]{:S(2)}, u32[]{:S(2)}) collective-permute-start(bf16[16,1600]{1,0:T(8,128)(2,1)S(1)} %get-tuple-element.5), channel_id=1, source_target_pairs={{1,0},{2,1},{3,2},{4,3},{5,4},{6,5},{7,6},{8,7},{9,8},{10,9},{11,1... | collective-permute-start | bytes 153608 | tf_op jit(solution)/shard_map/ppermute | solution.py:190
  19.4 23.4 %collective-permute-start = (bf16[16,1600]{1,0:T(8,128)(2,1)S(1)}, bf16[16,1600]{1,0:T(8,128)(2,1)S(1)}, u32[]{:S(2)}, u32[]{:S(2)}) collective-permute-start(bf16[16,1600]{1,0:T(8,128)(2,1)S(1)} %get-tuple-element.6), channel_id=1, source_target_pairs={{0,1},{1,2},{2,3},{3,4},{4,5},{5,6},{6,7},{7,8},{8,9},{9,10},{10,1... | collective-permute-start | bytes 153608 | tf_op jit(solution)/shard_map/ppermute | solution.py:189
  43.9 1.2 copy-start.1
  114.1 1.3 copy-start
  115.4 30.6 %all-to-all-start.2 = ((bf16[8,240,512]{2,1,0:T(8,128)(2,1)}), bf16[8,240,512]{2,1,0:T(8,128)(2,1)S(1)}, u32[]{:S(2)}, u32[]{:S(2)}) async-start(bf16[8,240,512]{2,1,0:T(8,128)(2,1)} %bitcast.8), calls=%async_computation.2 | async-start | bytes 3932160 | tf_op jit(solution)/shard_map/all_to_all | solution.py:201
where the time goes:
time: 157 us
  blocking collectives  54.5 us (35%)
  waiting for transfers between devices  47.7 us (30%)
  Pallas kernels  36.8 us (23%)
  starting transfers between devices  12.1 us (8%)
  local copies, waits for them, and re-layouts  5.77 us (4%)
    all_to_all x1, blocking collectives, on_device(): lax.all_to_all(blended.reshape(patches, per_source, entries), 'grid', spl...  54.5 us
    all_to_all x1, waiting for transfers between devices, on_device(): lax.all_to_all(result.reshape(groups, own_members * quantities, columns),...  24.8 us
    ppermute x1, waiting for transfers between devices, on_device(): right = lax.ppermute(turned[:RIM], 'grid', preceding)  21.2 us
    pallas_call x1, Pallas kernels, update(): pl.pallas_call(update_kernel, grid=(columns // lanes,), in_specs=[pl.Bloc...  14.4 us
    pallas_call x1, Pallas kernels, pick_columns(): pl.pallas_call(pick_kernel, grid=(groups,), in_specs=[full_spec((rows, ce...  10.5 us
    pallas_call x1, Pallas kernels, place_columns(): pl.pallas_call(place_kernel, grid=(groups,), in_specs=[full_spec(parts.sh...  10.4 us
    all_to_all x1, starting transfers between devices, on_device(): lax.all_to_all(chosen, 'member', split_axis=0, concat_axis=0, tiled=True)  5.81 us
    all_to_all x1, starting transfers between devices, on_device(): lax.all_to_all(result.reshape(groups, own_members * quantities, columns),...  5.7 us
  transfers between devices with their start and end apart: 4, of which 3 were waited for; matrix products, arithmetic and copies ran while one was open for 0% of the time, Pallas kernels for 1%

commit v1 on v0

v1 whole, which is shorter than its diff:
```python
import functools

import jax
import jax.numpy as jnp
from jax import lax
from jax.experimental import pallas as pl
from jax.experimental.pallas import tpu as pltpu
from jax.sharding import PartitionSpec as P


ENSEMBLE_SIZE = 40
RIM = 16
LANES = 128
MIB = 1024 * 1024
STEPS = [2, 6, 7, 5, 3, 1, 4, 0]
TOGETHER = 2
PLACED = 4


def cost(flops, moved):
    return pl.CostEstimate(flops=int(flops), bytes_accessed=int(moved), transcendentals=0)


def full_spec(shape):
    return pl.BlockSpec(shape, lambda *_: (0,) * len(shape))


def pick_kernel(rows_ref, targets_ref, out_ref):
    cells = rows_ref.shape[1]
    columns = targets_ref.shape[1]
    cell_ids = lax.broadcasted_iota(jnp.int32, (cells, columns), 0)
    onehot = jnp.where(cell_ids == targets_ref[...], 1.0, 0.0).astype(jnp.bfloat16)
    out_ref[...] = jnp.dot(
        rows_ref[...], onehot, preferred_element_type=jnp.float32
    ).astype(jnp.bfloat16)


def pick_columns(source_rows, targets):
    rows, cells = source_rows.shape
    columns = targets.shape[1]
    return pl.pallas_call(
        pick_kernel,
        out_shape=jax.ShapeDtypeStruct((rows, columns), jnp.bfloat16),
        compiler_params=pltpu.CompilerParams(vmem_limit_bytes=24 * MIB),
        cost_estimate=cost(2 * rows * cells * columns, 2 * rows * columns),
        name="pick",
    )(source_rows, targets)


def place_kernel(*refs, count, more):
    part_refs, positions_ref = refs[:count], refs[count]
    out_ref = refs[-1]
    block = out_ref.shape[1]
    parts = jnp.concatenate([ref[...] for ref in part_refs], axis=1)
    wide = jnp.concatenate([positions_ref[...]] * (block // LANES), axis=1)
    first = pl.program_id(0) * block
    target_ids = first + lax.broadcasted_iota(jnp.int32, wide.shape, 1)
    onehot = jnp.where(wide == target_ids, 1.0, 0.0).astype(jnp.bfloat16)
    placed = jnp.dot(parts, onehot, preferred_element_type=jnp.float32)
    if more:
        placed = placed + refs[count + 1][...].astype(jnp.float32)
    out_ref[...] = placed.astype(jnp.bfloat16)


def place_columns(parts, positions, before, cells):
    rows, columns = parts[0].shape
    block = 512
    more = before is not None
    block_spec = pl.BlockSpec((rows, block), lambda i: (0, i))
    operands = [*parts, positions]
    specs = [full_spec(operand.shape) for operand in operands]
    if more:
        operands.append(before)
        specs.append(block_spec)
    return pl.pallas_call(
        functools.partial(place_kernel, count=len(parts), more=more),
        grid=(cells // block,),
        in_specs=specs,
        out_specs=block_spec,
        out_shape=jax.ShapeDtypeStruct((rows, cells), jnp.bfloat16),
        compiler_params=pltpu.CompilerParams(vmem_limit_bytes=32 * MIB),
        cost_estimate=cost(2 * rows * cells * columns * len(parts), 4 * rows * cells),
        name="place",
    )(*operands)


def turn_kernel(transforms_ref, out_ref):
    out_ref[...] = jnp.transpose(transforms_ref[...]).astype(jnp.bfloat16)


def turn(transforms):
    entries, points = transforms.shape
    return pl.pallas_call(
        turn_kernel,
        out_shape=jax.ShapeDtypeStruct((points, entries), jnp.bfloat16),
        compiler_params=pltpu.CompilerParams(vmem_limit_bytes=24 * MIB),
        cost_estimate=cost(1e8, 6 * entries * points),
        name="turn",
    )(transforms)


def blend_kernel(left_ref, own_ref, right_ref, points_ref, factors_ref, out_ref):
    rim, points_own = left_ref.shape[0], own_ref.shape[0]
    columns = points_ref.shape[2]
    extent = points_own + 2 * rim
    factors = [factors_ref[which] for which in range(3)]
    total = factors[0] + factors[1] + factors[2]
    shares = [factor / total for factor in factors]
    slot_ids = lax.broadcasted_iota(jnp.int32, (extent, columns), 0)
    spread = jnp.zeros((extent, columns), jnp.float32)
    for which in range(3):
        spread = spread + jnp.where(
            points_ref[which] == slot_ids, shares[which], 0.0
        )
    high = spread.astype(jnp.bfloat16)
    low = (spread - high.astype(jnp.float32)).astype(jnp.bfloat16)
    widened = jnp.concatenate([left_ref[...], own_ref[...], right_ref[...]], axis=0)
    dims = (((0,), (0,)), ((), ()))
    out_ref[...] = lax.dot_general(
        jnp.concatenate([high, low], axis=0),
        jnp.concatenate([widened, widened], axis=0),
        dims,
        preferred_element_type=jnp.float32,
    ).astype(jnp.bfloat16)


def blend(left, own, right, points, factors):
    return pl.pallas_call(
        blend_kernel,
        out_shape=jax.ShapeDtypeStruct((points.shape[2], own.shape[1]), jnp.bfloat16),
        compiler_params=pltpu.CompilerParams(vmem_limit_bytes=24 * MIB),
        cost_estimate=cost(1e9, 4e6),
        name="blend",
    )(left, own, right, points, factors)


def center_kernel(*refs):
    *field_refs, deviation_ref, mean_ref = refs
    own = field_refs[0].shape[0]
    total = jnp.zeros(mean_ref.shape, jnp.float32)
    for ref in field_refs:
        for k in range(own):
            total = total + ref[k].astype(jnp.float32)
    mean = total * (1.0 / ENSEMBLE_SIZE)
    mean_ref[...] = mean
    for s, ref in enumerate(field_refs):
        for k in range(own):
            deviation_ref[s * own + k] = (ref[k].astype(jnp.float32) - mean).astype(jnp.bfloat16)


def center(fields):
    own, quantities, columns = fields[0].shape
    block = lambda i: (0, 0, i)
    return pl.pallas_call(
        center_kernel,
        grid=(columns // LANES,),
        in_specs=[pl.BlockSpec((own, quantities, LANES), block)] * len(fields),
        out_specs=[
            pl.BlockSpec((ENSEMBLE_SIZE, quantities, LANES), block),
            pl.BlockSpec((quantities, LANES), lambda i: (0, i)),
        ],
        out_shape=[
            jax.ShapeDtypeStruct((ENSEMBLE_SIZE, quantities, columns), jnp.bfloat16),
            jax.ShapeDtypeStruct((quantities, columns), jnp.float32),
        ],
        compiler_params=pltpu.CompilerParams(vmem_limit_bytes=24 * MIB),
        cost_estimate=cost(1e9, 4e6),
        name="center",
    )(*fields)


def tip_kernel(weights_ref, out_ref):
    out_ref[0] = jnp.transpose(weights_ref[...].astype(jnp.float32))


def tip(weights):
    columns, entries = weights.shape
    return pl.pallas_call(
        tip_kernel,
        grid=(columns // LANES,),
        in_specs=[pl.BlockSpec((LANES, entries), lambda i: (i, 0))],
        out_specs=pl.BlockSpec((1, entries, LANES), lambda i: (i, 0, 0)),
        out_shape=jax.ShapeDtypeStruct((columns // LANES, entries, LANES), jnp.float32),
        compiler_params=pltpu.CompilerParams(vmem_limit_bytes=24 * MIB),
        cost_estimate=cost(1e9, 4e6),
        name="tip",
    )(weights)


def update_kernel(group_ref, weights_ref, deviation_ref, mean_ref, *out_refs, steps):
    own = out_refs[0].shape[0]
    groups = ENSEMBLE_SIZE // own
    for step, out_ref in zip(steps, out_refs):
        first = group_ref[step] * own
        sums = [mean_ref[...] for _ in range(own)]
        for s in range(groups):
            start = group_ref[s] * (own * ENSEMBLE_SIZE) + first
            for k in range(own):
                deviation = deviation_ref[s * own + k].astype(jnp.float32)
                for j in range(own):
                    weight = weights_ref[0, pl.ds(start + k * ENSEMBLE_SIZE + j, 1), :]
                    sums[j] = sums[j] + deviation * weight
        for j in range(own):
            out_ref[j] = sums[j].astype(jnp.bfloat16)


def update(group, steps, weights, deviation, mean):
    members, quantities, columns = deviation.shape
    own = ENSEMBLE_SIZE // group.shape[0]
    block = lambda i, *_: (0, 0, i)
    return pl.pallas_call(
        functools.partial(update_kernel, steps=tuple(steps)),
        grid_spec=pltpu.PrefetchScalarGridSpec(
            num_scalar_prefetch=1,
            grid=(columns // LANES,),
            in_specs=[
                pl.BlockSpec((1, weights.shape[1], LANES), lambda i, *_: (i, 0, 0)),
                pl.BlockSpec((members, quantities, LANES), block),
                pl.BlockSpec((quantities, LANES), lambda i, *_: (0, i)),
            ],
            out_specs=[pl.BlockSpec((own, quantities, LANES), block)] * len(steps),
        ),
        out_shape=[jax.ShapeDtypeStruct((own, quantities, columns), jnp.bfloat16)] * len(steps),
        compiler_params=pltpu.CompilerParams(vmem_limit_bytes=24 * MIB),
        cost_estimate=cost(3e9 * len(steps), 8e6),
        name="update",
    )(group, weights, deviation, mean)


def exchange(part, s, groups):
    if s == 0:
        return part
    return lax.ppermute(part, "member", [(i, i ^ s) for i in range(groups)])


def local_step(
    prior_ensemble, domain_site_mapping, neighbour_triples, stencil_factors, sparse_node_transforms
):
    own_members, quantities, cells = prior_ensemble.shape
    groups = lax.axis_size("member")
    patches = lax.axis_size("grid")
    columns = cells // groups
    per_source = columns // patches
    entries = ENSEMBLE_SIZE * ENSEMBLE_SIZE
    rows = own_members * quantities

    turned = turn(sparse_node_transforms)
    following = [(i, (i + 1) % patches) for i in range(patches)]
    preceding = [((i + 1) % patches, i) for i in range(patches)]
    left = lax.ppermute(turned[-RIM:], "grid", following)
    right = lax.ppermute(turned[:RIM], "grid", preceding)
    blended = blend(
        left,
        turned,
        right,
        jnp.transpose(neighbour_triples, (1, 0, 2)),
        jnp.transpose(stencil_factors, (1, 0, 2)),
    )
    weights = lax.all_to_all(
        blended.reshape(patches, per_source, entries),
        "grid",
        split_axis=0,
        concat_axis=0,
        tiled=True,
    ).reshape(columns, entries)

    group = (lax.axis_index("member") ^ jnp.arange(groups, dtype=jnp.int32)).astype(jnp.int32)
    order = jnp.transpose(domain_site_mapping, (1, 0, 2)).reshape(groups, columns)[group]
    source_rows = prior_ensemble.reshape(rows, cells)
    steps = STEPS
    fields = [None] * groups
    for s in steps:
        chosen = pick_columns(source_rows, order[s : s + 1])
        fields[s] = exchange(chosen, s, groups).reshape(own_members, quantities, columns)
    deviation, mean = center(fields)
    spread = tip(weights)
    positions = jnp.broadcast_to(order[jnp.array(steps)].reshape(cells, 1), (cells, LANES))
    results = []
    for first in range(0, groups, TOGETHER):
        now = steps[first : first + TOGETHER]
        parts = update(group, now, spread, deviation, mean)
        for s, part in zip(now, parts):
            results.append(exchange(part.reshape(rows, columns), s, groups))
    placed = None
    for first in range(0, groups, PLACED):
        placed = place_columns(
            results[first : first + PLACED],
            positions[first * columns : (first + PLACED) * columns],
            placed,
            cells,
        )
    return placed.reshape(own_members, quantities, cells)


def solution(mesh):
    return jax.shard_map(
        local_step,
        mesh=mesh,
        in_specs=(
            P("member", None, "grid"),
            P(None, None, "grid"),
            P("grid", None, "member"),
            P("grid", None, "member"),
            P(None, "grid"),
        ),
        out_specs=P("member", None, "grid"),
        check_vma=False,
    )
```

time: 157 us -> 128 us (0.82)
  blocking collectives: 54.5 us -> 0 us
  starting transfers between devices: 12.1 us -> 41 us
  waiting for transfers between devices: 47.7 us -> 29.9 us
  Pallas kernels: 36.8 us -> 45.6 us
  local copies, waits for them, and re-layouts: 5.77 us -> 9.68 us
    all_to_all x1 -> x0, blocking collectives: 54.5 us -> none  [on_device(): lax.all_to_all(blended.reshape(patches, per_source, entries), 'grid', spl...]
    ppermute x2 -> x16, starting transfers between devices: 0.59 us -> 26.3 us  [the longest x14 22.9 us: exchange(): return lax.ppermute(part, 'member', [(i, i ^ s) for i in range(groups)])]
    all_to_all x2 -> x1, waiting for transfers between devices: 24.8 us -> 0.01 us  [local_step(): lax.all_to_all(blended.reshape(patches, per_source, entries), 'grid', spl...]
    pallas_call x3 -> x16, Pallas kernels: 35.4 us -> 43 us  [the longest x4 17.1 us: update(): pl.pallas_call(functools.partial(update_kernel, steps=tuple(steps)), grid...]
    ppermute x2 -> x16, waiting for transfers between devices: 22.9 us -> 29.9 us  [the longest x14 28.1 us: exchange(): return lax.ppermute(part, 'member', [(i, i ^ s) for i in range(groups)])]
    unnamed x14 -> x21, local copies, waits for them, and re-layouts: 4.03 us -> 7.68 us
    all_to_all x2 -> x1, starting transfers between devices: 11.5 us -> 14.8 us  [local_step(): lax.all_to_all(blended.reshape(patches, per_source, entries), 'grid', spl...]
  transfers between devices with their start and end apart: 4 -> 17, of which waited for: 3 -> 4; matrix products, arithmetic and copies ran while one was open for 0% -> 1% of each run, Pallas kernels for 1% -> 18%
where the time goes in v1:
time: 128 us; the launch traced here: 127 us
  Pallas kernels  45.6 us (36%)
  starting transfers between devices  41 us (32%)
  waiting for transfers between devices  29.9 us (23%)
  local copies, waits for them, and re-layouts  9.68 us (8%)
    ppermute x14, waiting for transfers between devices, exchange(): return lax.ppermute(part, 'member', [(i, i ^ s) for i in range(groups)])  28.1 us
    ppermute x14, starting transfers between devices, exchange(): return lax.ppermute(part, 'member', [(i, i ^ s) for i in range(groups)])  22.9 us
    pallas_call x4, Pallas kernels, update(): pl.pallas_call(functools.partial(update_kernel, steps=tuple(steps)), grid...  17.1 us
    all_to_all x1, starting transfers between devices, local_step(): lax.all_to_all(blended.reshape(patches, per_source, entries), 'grid', spl...  14.8 us
    pallas_call x2, Pallas kernels, place_columns(): pl.pallas_call(functools.partial(place_kernel, count=len(parts), more=mor...  11.9 us
    pallas_call x8, Pallas kernels, pick_columns(): pl.pallas_call(pick_kernel, out_shape=jax.ShapeDtypeStruct((rows, columns...  11.8 us
    unnamed x21, local copies, waits for them, and re-layouts  7.68 us
    ppermute x1, starting transfers between devices, local_step(): right = lax.ppermute(turned[:RIM], 'grid', preceding)  3.24 us
  transfers between devices with their start and end apart: 17, of which 4 were waited for; matrix products, arithmetic and copies ran while one was open for 1% of the time, Pallas kernels for 18%

profile of v1, /device:TPU:30, one launch (start us, length us, event | category | flops | bytes accessed | tf_op | source)
XLA Modules:
  0.0 126.6 jit_solution(16982200921354491181)
XLA Ops:
  0.0 1.1 copy-done
  1.1 0.2 turn.1.own_ref
  1.4 0.1 collective-permute-start
  1.5 3.2 %collective-permute-start.1 = (bf16[16,1600]{1,0:T(8,128)(2,1)S(1)}, bf16[16,1600]{1,0:T(8,128)(2,1)S(1)}, u32[]{:S(2)}, u32[]{:S(2)}) collective-permute-start(bf16[16,1600]{1,0:T(8,128)(2,1)S(1)} %get-tuple-element.25), channel_id=1, source_target_pairs={{1,0},{2,1},{3,2},{4,3},{5,4},{6,5},{7,6},{8,7},{9,8},{10,9},{11,1... | collective-permute-start | bytes 153608 | tf_op jit(solution)/shard_map/ppermute | solution.py:251
  4.7 1.8 %collective-permute-done.left_ref = bf16[16,1600]{1,0:T(8,128)(2,1)S(1)} collective-permute-done((bf16[16,1600]{1,0:T(8,128)(2,1)S(1)}, bf16[16,1600]{1,0:T(8,128)(2,1)S(1)}, u32[]{:S(2)}, u32[]{:S(2)}) %collective-permute-start) | collective-permute-done | bytes 51232 | tf_op jit(solution)/shard_map/ppermute | solution.py:250
  6.5 0.0 collective-permute-done.1.right_ref
  6.5 0.7 copy-done.3
  7.2 0.7 copy-done.4
  7.9 2.4 %blend.1 = bf16[512,1600]{1,0:T(8,128)(2,1)} custom-call(bf16[16,1600]{1,0:T(8,128)(2,1)S(1)} %collective-permute-done.left_ref, bf16[128,1600]{1,0:T(8,128)(2,1)S(1)} %turn.1.own_ref, bf16[16,1600]{1,0:T(8,128)(2,1)S(1)} %collective-permute-done.1.right_ref, s32[3,1,512]{2,1,0:T(1,128)S(1)} %bitcast.54, f32[3,1,512]{2,1,0:T(1,128)S(1)} %bitcast.55), custom_call_target="tpu_custom_call" | custom-call | flops 1000000000 | bytes 4000000 | tf_op jit(solution)/shard_map/blend/pallas_call | solution.py:128
  10.3 14.8 %all-to-all-start = ((bf16[32,16,1600]{2,1,0:T(8,128)(2,1)}), bf16[32,16,1600]{2,1,0:T(8,128)(2,1)S(1)}, u32[]{:S(2)}, u32[]{:S(2)}) async-start(bf16[32,16,1600]{2,1,0:T(8,128)(2,1)} %bitcast.2), calls=%async_computation | async-start | bytes 3407872 | tf_op jit(solution)/shard_map/all_to_all | solution.py:259
  25.1 0.1 copy.8
  25.2 0.1 reshape.86
  25.3 0.6 gather_fusion
  25.9 0.0 copy-start.1
  25.9 1.5 %copy-done.1 = bf16[5,48,4096]{2,1,0:T(8,128)(2,1)S(1)} copy-done((bf16[5,48,4096]{2,1,0:T(8,128)(2,1)S(1)}, bf16[5,48,4096]{2,1,0:T(8,128)(2,1)}, u32[]{:S(2)}) %copy-start.1) | copy-done | bytes 1966104
  27.5 1.9 %pick.9 = bf16[240,512]{1,0:T(8,128)(2,1)} custom-call(bf16[240,4096]{1,0:T(8,128)(2,1)S(1)} %bitcast.32, s32[1,512]{1,0:T(1,128)S(1)} %get-tuple-element.35.targets_ref), custom_call_target="tpu_custom_call" | custom-call | flops 1006632960 | bytes 245760 | tf_op jit(solution)/shard_map/pick/pallas_call | solution.py:41
  29.4 0.8 collective-permute-start.2
  30.2 1.9 %pick.10 = bf16[240,512]{1,0:T(8,128)(2,1)} custom-call(bf16[240,4096]{1,0:T(8,128)(2,1)S(1)} %bitcast.33, s32[1,512]{1,0:T(1,128)S(1)} %get-tuple-element.34.targets_ref), custom_call_target="tpu_custom_call" | custom-call | flops 1006632960 | bytes 245760 | tf_op jit(solution)/shard_map/pick/pallas_call | solution.py:41
  32.1 1.1 collective-permute-start.3
  33.2 1.2 pick.11
  34.4 2.8 %collective-permute-start.4 = (bf16[240,512]{1,0:T(8,128)(2,1)S(1)}, bf16[240,512]{1,0:T(8,128)(2,1)S(1)}, u32[]{:S(2)}, u32[]{:S(2)}) collective-permute-start(bf16[240,512]{1,0:T(8,128)(2,1)S(1)} %pick.11), channel_id=1, source_target_pairs={{0,96},{32,64},{64,32},{96,0},{128,224},{160,192},{192,160},{224,1... | collective-permute-start | bytes 737288 | tf_op jit(solution)/shard_map/ppermute | solution.py:233
  37.3 1.2 pick.12
  38.5 0.0 copy-start.8
  38.5 0.1 collective-permute-start.5
  38.6 1.9 %pick.13 = bf16[240,512]{1,0:T(8,128)(2,1)} custom-call(bf16[240,4096]{1,0:T(8,128)(2,1)S(1)} %bitcast.36, s32[1,512]{1,0:T(1,128)S(1)} %get-tuple-element.31.targets_ref), custom_call_target="tpu_custom_call" | custom-call | flops 1006632960 | bytes 245760 | tf_op jit(solution)/shard_map/pick/pallas_call | solution.py:41
  40.5 1.1 collective-permute-start.6
  41.6 0.6 gather_fusion.1
  42.2 0.0 copy-start.2
  42.2 1.5 %copy-done.2 = bf16[5,48,4096]{2,1,0:T(8,128)(2,1)S(1)} copy-done((bf16[5,48,4096]{2,1,0:T(8,128)(2,1)S(1)}, bf16[5,48,4096]{2,1,0:T(8,128)(2,1)}, u32[]{:S(2)}) %copy-start.2) | copy-done | bytes 1966104
  43.7 1.2 pick.14
  45.0 1.2 pick.15
  46.2 1.9 %collective-permute-start.7 = (bf16[240,512]{1,0:T(8,128)(2,1)S(1)}, bf16[240,512]{1,0:T(8,128)(2,1)S(1)}, u32[]{:S(2)}, u32[]{:S(2)}) collective-permute-start(bf16[240,512]{1,0:T(8,128)(2,1)S(1)} %pick.14), channel_id=1, source_target_pairs={{0,192},{32,224},{64,128},{96,160},{128,64},{160,96},{192,0},{224,... | collective-permute-start | bytes 737288 | tf_op jit(solution)/shard_map/ppermute | solution.py:233
  48.1 0.0 collective-permute-done.3
  48.1 4.2 %collective-permute-start.8 = (bf16[240,512]{1,0:T(8,128)(2,1)S(1)}, bf16[240,512]{1,0:T(8,128)(2,1)S(1)}, u32[]{:S(2)}, u32[]{:S(2)}) collective-permute-start(bf16[240,512]{1,0:T(8,128)(2,1)S(1)} %pick.15), channel_id=1, source_target_pairs={{0,224},{32,192},{64,160},{96,128},{128,96},{160,64},{192,32},{224... | collective-permute-start | bytes 737288 | tf_op jit(solution)/shard_map/ppermute | solution.py:233
  52.3 1.2 pick.8
  53.5 0.0 collective-permute-done.4
  53.5 17.1 %collective-permute-done.5 = bf16[240,512]{1,0:T(8,128)(2,1)S(1)} collective-permute-done((bf16[240,512]{1,0:T(8,128)(2,1)S(1)}, bf16[240,512]{1,0:T(8,128)(2,1)S(1)}, u32[]{:S(2)}, u32[]{:S(2)}) %collective-permute-start.5) | collective-permute-done | bytes 245792 | tf_op jit(solution)/shard_map/ppermute | solution.py:233
  70.7 0.0 collective-permute-done.6
  70.7 0.0 collective-permute-done.7
  70.7 0.0 collective-permute-done.8
  70.7 1.4 %center.1 = (bf16[40,48,512]{2,1,0:T(8,128)(2,1)S(1)}, f32[48,512]{1,0:T(8,128)S(1)}) custom-call(bf16[5,48,512]{2,1,0:T(8,128)(2,1)S(1)} %bitcast.57, bf16[5,48,512]{2,1,0:T(8,128)(2,1)S(1)} %bitcast.40, bf16[5,48,512]{2,1,0:T(8,128)(2,1)S(1)} %bitcast.41, bf16[5,48,512]{2,1,0:T(8,128)(2,1)S(1)} %bitcast.42, bf16[5,48,512]{2,1,0:T(8,128)(2,1)S(1)} %bitcast.44, ...), custom_call_target="tpu_custom_call" | custom-call | flops 1000000000 | bytes 4000000 | tf_op jit(solution)/shard_map/center/pallas_call | solution.py:154
  72.1 0.0 copy-start.5
  72.1 1.3 copy-done.5
  73.4 0.0 all-to-all-done
  73.4 0.8 tip.1.weights_ref
  74.2 0.8 copy-done.6
  74.9 4.3 %update.4 = (bf16[5,48,512]{2,1,0:T(8,128)(2,1)S(1)}, bf16[5,48,512]{2,1,0:T(8,128)(2,1)S(1)}) custom-call(s32[8]{0:T(128)S(1)} %iota_xor_fusion.group_ref, f32[4,1600,128]{2,1,0:T(8,128)S(1)} %tip.1.weights_ref, bf16[40,48,512]{2,1,0:T(8,128)(2,1)S(1)} %copy-done.6, f32[48,512]{1,0:T(8,128)S(1)} %get-tuple-element.16.mean_ref), custom_call_target="tpu_custom_call" | custom-call | flops 6000000000 | bytes 8000000 | tf_op jit(solution)/shard_map/update/pallas_call | solution.py:211
  79.2 4.3 %update.6 = (bf16[5,48,512]{2,1,0:T(8,128)(2,1)S(1)}, bf16[5,48,512]{2,1,0:T(8,128)(2,1)S(1)}) custom-call(s32[8]{0:T(128)S(1)} %iota_xor_fusion.group_ref, f32[4,1600,128]{2,1,0:T(8,128)S(1)} %tip.1.weights_ref, bf16[40,48,512]{2,1,0:T(8,128)(2,1)S(1)} %copy-done.6, f32[48,512]{1,0:T(8,128)S(1)} %get-tuple-element.16.mean_ref), custom_call_target="tpu_custom_call" | custom-call | flops 6000000000 | bytes 8000000 | tf_op jit(solution)/shard_map/update/pallas_call | solution.py:211
  83.5 4.3 %update.7 = (bf16[5,48,512]{2,1,0:T(8,128)(2,1)S(1)}, bf16[5,48,512]{2,1,0:T(8,128)(2,1)S(1)}) custom-call(s32[8]{0:T(128)S(1)} %iota_xor_fusion.group_ref, f32[4,1600,128]{2,1,0:T(8,128)S(1)} %tip.1.weights_ref, bf16[40,48,512]{2,1,0:T(8,128)(2,1)S(1)} %copy-done.6, f32[48,512]{1,0:T(8,128)S(1)} %get-tuple-element.16.mean_ref), custom_call_target="tpu_custom_call" | custom-call | flops 6000000000 | bytes 8000000 | tf_op jit(solution)/shard_map/update/pallas_call | solution.py:211
  87.8 1.3 collective-permute-start.12
  89.1 3.5 %collective-permute-start.13 = (bf16[240,512]{1,0:T(8,128)(2,1)S(1)}, bf16[240,512]{1,0:T(8,128)(2,1)S(1)}, u32[]{:S(2)}, u32[]{:S(2)}) collective-permute-start(bf16[240,512]{1,0:T(8,128)(2,1)S(1)} %bitcast.52), channel_id=1, source_target_pairs={{0,192},{32,224},{64,128},{96,160},{128,64},{160,96},{192,0},{224,... | collective-permute-start | bytes 737288 | tf_op jit(solution)/shard_map/ppermute | solution.py:233
  92.5 0.3 collective-permute-start.14
  92.9 1.8 %collective-permute-start.15 = (bf16[240,512]{1,0:T(8,128)(2,1)S(1)}, bf16[240,512]{1,0:T(8,128)(2,1)S(1)}, u32[]{:S(2)}, u32[]{:S(2)}) collective-permute-start(bf16[240,512]{1,0:T(8,128)(2,1)S(1)} %bitcast.49), channel_id=1, source_target_pairs={{0,160},{32,128},{64,224},{96,192},{128,32},{160,0},{192,96},{224,... | collective-permute-start | bytes 737288 | tf_op jit(solution)/shard_map/ppermute | solution.py:233
  94.7 4.3 %update.5 = (bf16[5,48,512]{2,1,0:T(8,128)(2,1)S(1)}, bf16[5,48,512]{2,1,0:T(8,128)(2,1)S(1)}) custom-call(s32[8]{0:T(128)S(1)} %iota_xor_fusion.group_ref, f32[4,1600,128]{2,1,0:T(8,128)S(1)} %tip.1.weights_ref, bf16[40,48,512]{2,1,0:T(8,128)(2,1)S(1)} %copy-done.6, f32[48,512]{1,0:T(8,128)S(1)} %get-tuple-element.16.mean_ref), custom_call_target="tpu_custom_call" | custom-call | flops 6000000000 | bytes 8000000 | tf_op jit(solution)/shard_map/update/pallas_call | solution.py:211
  98.9 2.2 %collective-permute-start.9 = (bf16[240,512]{1,0:T(8,128)(2,1)S(1)}, bf16[240,512]{1,0:T(8,128)(2,1)S(1)}, u32[]{:S(2)}, u32[]{:S(2)}) collective-permute-start(bf16[240,512]{1,0:T(8,128)(2,1)S(1)} %bitcast.45), channel_id=1, source_target_pairs={{0,96},{32,64},{64,32},{96,0},{128,224},{160,192},{192,160},{224,1... | collective-permute-start | bytes 737288 | tf_op jit(solution)/shard_map/ppermute | solution.py:233
  101.1 0.0 collective-permute-done.12.refs_0_
  101.2 1.3 %collective-permute-start.10 = (bf16[240,512]{1,0:T(8,128)(2,1)S(1)}, bf16[240,512]{1,0:T(8,128)(2,1)S(1)}, u32[]{:S(2)}, u32[]{:S(2)}) collective-permute-start(bf16[240,512]{1,0:T(8,128)(2,1)S(1)} %bitcast.43), channel_id=1, source_target_pairs={{0,32},{32,0},{64,96},{96,64},{128,160},{160,128},{192,224},{224,1... | collective-permute-start | bytes 737288 | tf_op jit(solution)/shard_map/ppermute | solution.py:233
  102.5 3.7 %collective-permute-done.13.refs_1_ = bf16[240,512]{1,0:T(8,128)(2,1)S(1)} collective-permute-done((bf16[240,512]{1,0:T(8,128)(2,1)S(1)}, bf16[240,512]{1,0:T(8,128)(2,1)S(1)}, u32[]{:S(2)}, u32[]{:S(2)}) %collective-permute-start.13) | collective-permute-done | bytes 245792 | tf_op jit(solution)/shard_map/ppermute | solution.py:233
  106.2 0.5 collective-permute-start.11
  106.7 7.2 %collective-permute-done.14.refs_2_ = bf16[240,512]{1,0:T(8,128)(2,1)S(1)} collective-permute-done((bf16[240,512]{1,0:T(8,128)(2,1)S(1)}, bf16[240,512]{1,0:T(8,128)(2,1)S(1)}, u32[]{:S(2)}, u32[]{:S(2)}) %collective-permute-start.14) | collective-permute-done | bytes 245792 | tf_op jit(solution)/shard_map/ppermute | solution.py:233
  113.9 0.3 broadcast_in_dim.13.refs_4_
  114.3 5.5 %place.2.refs_5_ = bf16[240,4096]{1,0:T(8,128)(2,1)S(1)} custom-call(bf16[240,512]{1,0:T(8,128)(2,1)S(1)} %collective-permute-done.12.refs_0_, bf16[240,512]{1,0:T(8,128)(2,1)S(1)} %collective-permute-done.13.refs_1_, bf16[240,512]{1,0:T(8,128)(2,1)S(1)} %collective-permute-done.14.refs_2_, bf16[240,512]{1,0:T(8,128)(2,1)S(1)} %collective-permute-done.15.refs_3_, ...), custom_call_target="tpu_custom_call" | custom-call | flops 4026531840 | bytes 3932160 | tf_op jit(solution)/shard_map/place/pallas_call | solution.py:75
  119.9 0.3 broadcast_in_dim.12.refs_4_
  120.2 6.4 %place.3 = bf16[240,4096]{1,0:T(8,128)(2,1)} custom-call(bf16[240,512]{1,0:T(8,128)(2,1)S(1)} %collective-permute-done.9.refs_0_, bf16[240,512]{1,0:T(8,128)(2,1)S(1)} %collective-permute-done.10.refs_1_, bf16[240,512]{1,0:T(8,128)(2,1)S(1)} %collective-permute-done.11.refs_2_, bf16[240,512]{1,0:T(8,128)(2,1)S(1)} %bitcast.56, ...), custom_call_target="tpu_custom_call" | custom-call | flops 4026531840 | bytes 3932160 | tf_op jit(solution)/shard_map/place/pallas_call | solution.py:75
  (21 shorter events, 0.1 us)
Async XLA Ops:
  0.0 1.1 copy-start
  1.4 5.1 %collective-permute-start = (bf16[16,1600]{1,0:T(8,128)(2,1)S(1)}, bf16[16,1600]{1,0:T(8,128)(2,1)S(1)}, u32[]{:S(2)}, u32[]{:S(2)}) collective-permute-start(bf16[16,1600]{1,0:T(8,128)(2,1)S(1)} %get-tuple-element.26), channel_id=1, source_target_pairs={{0,1},{1,2},{2,3},{3,4},{4,5},{5,6},{6,7},{7,8},{8,9},{9,10},{10,1... | collective-permute-start | bytes 153608 | tf_op jit(solution)/shard_map/ppermute | solution.py:250
  1.5 5.1 %collective-permute-start.1 = (bf16[16,1600]{1,0:T(8,128)(2,1)S(1)}, bf16[16,1600]{1,0:T(8,128)(2,1)S(1)}, u32[]{:S(2)}, u32[]{:S(2)}) collective-permute-start(bf16[16,1600]{1,0:T(8,128)(2,1)S(1)} %get-tuple-element.25), channel_id=1, source_target_pairs={{1,0},{2,1},{3,2},{4,3},{5,4},{6,5},{7,6},{8,7},{9,8},{10,9},{11,1... | collective-permute-start | bytes 153608 | tf_op jit(solution)/shard_map/ppermute | solution.py:251
  6.5 0.7 copy-start.3
  7.2 0.7 copy-start.4
  10.3 14.8 %copy-start.7 = (s32[32,8,16]{0,2,1:T(8,128)S(1)}, s32[32,8,16]{0,2,1:T(8,128)}, u32[]{:S(2)}) copy-start(s32[32,8,16]{0,2,1:T(8,128)} %param.7) | copy-start | bytes 49156
  10.3 63.1 %all-to-all-start = ((bf16[32,16,1600]{2,1,0:T(8,128)(2,1)}), bf16[32,16,1600]{2,1,0:T(8,128)(2,1)S(1)}, u32[]{:S(2)}, u32[]{:S(2)}) async-start(bf16[32,16,1600]{2,1,0:T(8,128)(2,1)} %bitcast.2), calls=%async_computation | async-start | bytes 3407872 | tf_op jit(solution)/shard_map/all_to_all | solution.py:259
  25.9 1.5 %copy-start.1 = (bf16[5,48,4096]{2,1,0:T(8,128)(2,1)S(1)}, bf16[5,48,4096]{2,1,0:T(8,128)(2,1)}, u32[]{:S(2)}) copy-start(bf16[5,48,4096]{2,1,0:T(8,128)(2,1)} %param.6) | copy-start | bytes 5898244
  29.4 16.8 %collective-permute-start.2 = (bf16[240,512]{1,0:T(8,128)(2,1)}, bf16[240,512]{1,0:T(8,128)(2,1)S(1)}, u32[]{:S(2)}, u32[]{:S(2)}) collective-permute-start(bf16[240,512]{1,0:T(8,128)(2,1)} %pick.9), channel_id=1, source_target_pairs={{0,32},{32,0},{64,96},{96,64},{128,160},{160,128},{192,224},{224,1... | collective-permute-start | bytes 737288 | tf_op jit(solution)/shard_map/ppermute | solution.py:233
  32.1 16.0 %collective-permute-start.3 = (bf16[240,512]{1,0:T(8,128)(2,1)}, bf16[240,512]{1,0:T(8,128)(2,1)S(1)}, u32[]{:S(2)}, u32[]{:S(2)}) collective-permute-start(bf16[240,512]{1,0:T(8,128)(2,1)} %pick.10), channel_id=1, source_target_pairs={{0,64},{32,96},{64,0},{96,32},{128,192},{160,224},{192,128},{224,1... | collective-permute-start | bytes 737288 | tf_op jit(solution)/shard_map/ppermute | solution.py:233
  34.4 19.1 %collective-permute-start.4 = (bf16[240,512]{1,0:T(8,128)(2,1)S(1)}, bf16[240,512]{1,0:T(8,128)(2,1)S(1)}, u32[]{:S(2)}, u32[]{:S(2)}) collective-permute-start(bf16[240,512]{1,0:T(8,128)(2,1)S(1)} %pick.11), channel_id=1, source_target_pairs={{0,96},{32,64},{64,32},{96,0},{128,224},{160,192},{192,160},{224,1... | collective-permute-start | bytes 737288 | tf_op jit(solution)/shard_map/ppermute | solution.py:233
  38.5 3.1 %copy-start.8 = (s32[8]{0:T(128)S(1)}, s32[8]{0:T(128)}, u32[]{:S(2)}) copy-start(s32[8]{0:T(128)} %constant.21) | copy-start | bytes 100
  38.5 32.1 %collective-permute-start.5 = (bf16[240,512]{1,0:T(8,128)(2,1)S(1)}, bf16[240,512]{1,0:T(8,128)(2,1)S(1)}, u32[]{:S(2)}, u32[]{:S(2)}) collective-permute-start(bf16[240,512]{1,0:T(8,128)(2,1)S(1)} %pick.12), channel_id=1, source_target_pairs={{0,128},{32,160},{64,192},{96,224},{128,0},{160,32},{192,64},{224,... | collective-permute-start | bytes 737288 | tf_op jit(solution)/shard_map/ppermute | solution.py:233
  40.5 30.1 %collective-permute-start.6 = (bf16[240,512]{1,0:T(8,128)(2,1)}, bf16[240,512]{1,0:T(8,128)(2,1)S(1)}, u32[]{:S(2)}, u32[]{:S(2)}) collective-permute-start(bf16[240,512]{1,0:T(8,128)(2,1)} %pick.13), channel_id=1, source_target_pairs={{0,160},{32,128},{64,224},{96,192},{128,32},{160,0},{192,96},{224,... | collective-permute-start | bytes 737288 | tf_op jit(solution)/shard_map/ppermute | solution.py:233
  42.2 1.5 %copy-start.2 = (bf16[5,48,4096]{2,1,0:T(8,128)(2,1)S(1)}, bf16[5,48,4096]{2,1,0:T(8,128)(2,1)}, u32[]{:S(2)}) copy-start(bf16[5,48,4096]{2,1,0:T(8,128)(2,1)} %param.6) | copy-start | bytes 5898244
  46.2 24.5 %collective-permute-start.7 = (bf16[240,512]{1,0:T(8,128)(2,1)S(1)}, bf16[240,512]{1,0:T(8,128)(2,1)S(1)}, u32[]{:S(2)}, u32[]{:S(2)}) collective-permute-start(bf16[240,512]{1,0:T(8,128)(2,1)S(1)} %pick.14), channel_id=1, source_target_pairs={{0,192},{32,224},{64,128},{96,160},{128,64},{160,96},{192,0},{224,... | collective-permute-start | bytes 737288 | tf_op jit(solution)/shard_map/ppermute | solution.py:233
  48.1 22.6 %collective-permute-start.8 = (bf16[240,512]{1,0:T(8,128)(2,1)S(1)}, bf16[240,512]{1,0:T(8,128)(2,1)S(1)}, u32[]{:S(2)}, u32[]{:S(2)}) collective-permute-start(bf16[240,512]{1,0:T(8,128)(2,1)S(1)} %pick.15), channel_id=1, source_target_pairs={{0,224},{32,192},{64,160},{96,128},{128,96},{160,64},{192,32},{224... | collective-permute-start | bytes 737288 | tf_op jit(solution)/shard_map/ppermute | solution.py:233
  72.1 1.3 %copy-start.5 = (bf16[40,48,512]{2,1,0:T(8,128)(2,1)}, bf16[40,48,512]{2,1,0:T(8,128)(2,1)S(1)}, u32[]{:S(2)}) copy-start(bf16[40,48,512]{2,1,0:T(8,128)(2,1)S(1)} %get-tuple-element.15.deviation_ref) | copy-start | bytes 5898244
  73.4 1.5 %copy-start.6 = (bf16[40,48,512]{2,1,0:T(8,128)(2,1)S(1)}, bf16[40,48,512]{2,1,0:T(8,128)(2,1)}, u32[]{:S(2)}) copy-start(bf16[40,48,512]{2,1,0:T(8,128)(2,1)} %copy-done.5) | copy-start | bytes 5898244
  87.8 13.3 %collective-permute-start.12 = (bf16[240,512]{1,0:T(8,128)(2,1)S(1)}, bf16[240,512]{1,0:T(8,128)(2,1)S(1)}, u32[]{:S(2)}, u32[]{:S(2)}) collective-permute-start(bf16[240,512]{1,0:T(8,128)(2,1)S(1)} %bitcast.53), channel_id=1, source_target_pairs={{0,64},{32,96},{64,0},{96,32},{128,192},{160,224},{192,128},{224,1... | collective-permute-start | bytes 737288 | tf_op jit(solution)/shard_map/ppermute | solution.py:233
  89.1 17.1 %collective-permute-start.13 = (bf16[240,512]{1,0:T(8,128)(2,1)S(1)}, bf16[240,512]{1,0:T(8,128)(2,1)S(1)}, u32[]{:S(2)}, u32[]{:S(2)}) collective-permute-start(bf16[240,512]{1,0:T(8,128)(2,1)S(1)} %bitcast.52), channel_id=1, source_target_pairs={{0,192},{32,224},{64,128},{96,160},{128,64},{160,96},{192,0},{224,... | collective-permute-start | bytes 737288 | tf_op jit(solution)/shard_map/ppermute | solution.py:233
  92.5 21.4 %collective-permute-start.14 = (bf16[240,512]{1,0:T(8,128)(2,1)S(1)}, bf16[240,512]{1,0:T(8,128)(2,1)S(1)}, u32[]{:S(2)}, u32[]{:S(2)}) collective-permute-start(bf16[240,512]{1,0:T(8,128)(2,1)S(1)} %bitcast.50), channel_id=1, source_target_pairs={{0,224},{32,192},{64,160},{96,128},{128,96},{160,64},{192,32},{224... | collective-permute-start | bytes 737288 | tf_op jit(solution)/shard_map/ppermute | solution.py:233
  92.9 21.1 %collective-permute-start.15 = (bf16[240,512]{1,0:T(8,128)(2,1)S(1)}, bf16[240,512]{1,0:T(8,128)(2,1)S(1)}, u32[]{:S(2)}, u32[]{:S(2)}) collective-permute-start(bf16[240,512]{1,0:T(8,128)(2,1)S(1)} %bitcast.49), channel_id=1, source_target_pairs={{0,160},{32,128},{64,224},{96,192},{128,32},{160,0},{192,96},{224,... | collective-permute-start | bytes 737288 | tf_op jit(solution)/shard_map/ppermute | solution.py:233
  98.9 20.9 %collective-permute-start.9 = (bf16[240,512]{1,0:T(8,128)(2,1)S(1)}, bf16[240,512]{1,0:T(8,128)(2,1)S(1)}, u32[]{:S(2)}, u32[]{:S(2)}) collective-permute-start(bf16[240,512]{1,0:T(8,128)(2,1)S(1)} %bitcast.45), channel_id=1, source_target_pairs={{0,96},{32,64},{64,32},{96,0},{128,224},{160,192},{192,160},{224,1... | collective-permute-start | bytes 737288 | tf_op jit(solution)/shard_map/ppermute | solution.py:233
  101.2 18.7 %collective-permute-start.10 = (bf16[240,512]{1,0:T(8,128)(2,1)S(1)}, bf16[240,512]{1,0:T(8,128)(2,1)S(1)}, u32[]{:S(2)}, u32[]{:S(2)}) collective-permute-start(bf16[240,512]{1,0:T(8,128)(2,1)S(1)} %bitcast.43), channel_id=1, source_target_pairs={{0,32},{32,0},{64,96},{96,64},{128,160},{160,128},{192,224},{224,1... | collective-permute-start | bytes 737288 | tf_op jit(solution)/shard_map/ppermute | solution.py:233
  106.2 13.7 %collective-permute-start.11 = (bf16[240,512]{1,0:T(8,128)(2,1)S(1)}, bf16[240,512]{1,0:T(8,128)(2,1)S(1)}, u32[]{:S(2)}, u32[]{:S(2)}) collective-permute-start(bf16[240,512]{1,0:T(8,128)(2,1)S(1)} %bitcast.47), channel_id=1, source_target_pairs={{0,128},{32,160},{64,192},{96,224},{128,0},{160,32},{192,64},{224,... | collective-permute-start | bytes 737288 | tf_op jit(solution)/shard_map/ppermute | solution.py:233

commit v2 on v1

v2 whole, which is shorter than its diff:
```python
import functools

import jax
import jax.numpy as jnp
from jax import lax
from jax.experimental import pallas as pl
from jax.experimental.pallas import tpu as pltpu
from jax.sharding import PartitionSpec as P


ENSEMBLE_SIZE = 40
RIM = 16
LANES = 128
MIB = 1024 * 1024
STEPS = [6, 7, 5, 4, 2, 3, 1, 0]
TOGETHER = 2


def cost(flops, moved):
    return pl.CostEstimate(flops=int(flops), bytes_accessed=int(moved), transcendentals=0)


def pick_kernel(rows_ref, targets_ref, out_ref):
    cells = rows_ref.shape[1]
    columns = targets_ref.shape[1]
    cell_ids = lax.broadcasted_iota(jnp.int32, (cells, columns), 0)
    onehot = jnp.where(cell_ids == targets_ref[...], 1.0, 0.0).astype(jnp.bfloat16)
    out_ref[...] = jnp.dot(
        rows_ref[...], onehot, preferred_element_type=jnp.float32
    ).astype(jnp.bfloat16)


def pick_columns(source_rows, targets):
    rows, cells = source_rows.shape
    columns = targets.shape[1]
    return pl.pallas_call(
        pick_kernel,
        out_shape=jax.ShapeDtypeStruct((rows, columns), jnp.bfloat16),
        compiler_params=pltpu.CompilerParams(vmem_limit_bytes=24 * MIB),
        cost_estimate=cost(2 * rows * cells * columns, 2 * rows * columns),
        name="pick",
    )(source_rows, targets)


def place_kernel(*refs):
    *part_refs, positions_ref, out_ref, rows_ref = refs
    columns = part_refs[0].shape[1]
    block = out_ref.shape[1]
    step = pl.program_id(0)

    @pl.when(step == 0)
    def _():
        for at, ref in enumerate(part_refs):
            rows_ref[:, at * columns : (at + 1) * columns] = ref[...]

    wide = jnp.concatenate([positions_ref[...]] * (block // LANES), axis=1)
    target_ids = step * block + lax.broadcasted_iota(jnp.int32, wide.shape, 1)
    onehot = jnp.where(wide == target_ids, 1.0, 0.0).astype(jnp.bfloat16)
    out_ref[...] = jnp.dot(
        rows_ref[...], onehot, preferred_element_type=jnp.float32
    ).astype(jnp.bfloat16)


def place_columns(parts, positions):
    rows, columns = parts[0].shape
    cells = columns * len(parts)
    block = 512
    whole = pl.BlockSpec(memory_space=pltpu.VMEM)
    return pl.pallas_call(
        place_kernel,
        grid=(cells // block,),
        in_specs=[whole] * (len(parts) + 1),
        out_specs=pl.BlockSpec((rows, block), lambda i: (0, i)),
        out_shape=jax.ShapeDtypeStruct((rows, cells), jnp.bfloat16),
        scratch_shapes=[pltpu.VMEM((rows, cells), jnp.bfloat16)],
        compiler_params=pltpu.CompilerParams(vmem_limit_bytes=24 * MIB),
        cost_estimate=cost(2 * rows * cells * cells, 4 * rows * cells),
        name="place",
    )(*parts, positions)


def turn_kernel(transforms_ref, out_ref):
    out_ref[...] = jnp.transpose(transforms_ref[...]).astype(jnp.bfloat16)


def turn(transforms):
    entries, points = transforms.shape
    return pl.pallas_call(
        turn_kernel,
        out_shape=jax.ShapeDtypeStruct((points, entries), jnp.bfloat16),
        compiler_params=pltpu.CompilerParams(vmem_limit_bytes=24 * MIB),
        cost_estimate=cost(1e8, 6 * entries * points),
        name="turn",
    )(transforms)


def weigh_kernel(points_ref, factors_ref, out_ref):
    extent, columns = out_ref.shape[0] // 2, out_ref.shape[1]
    factors = [factors_ref[which] for which in range(3)]
    total = factors[0] + factors[1] + factors[2]
    slot_ids = lax.broadcasted_iota(jnp.int32, (extent, columns), 0)
    spread = jnp.zeros((extent, columns), jnp.float32)
    for which in range(3):
        spread = spread + jnp.where(points_ref[which] == slot_ids, factors[which] / total, 0.0)
    high = spread.astype(jnp.bfloat16)
    out_ref[:extent] = high
    out_ref[extent:] = (spread - high.astype(jnp.float32)).astype(jnp.bfloat16)


def weigh(points, factors, extent):
    return pl.pallas_call(
        weigh_kernel,
        out_shape=jax.ShapeDtypeStruct((2 * extent, points.shape[2]), jnp.bfloat16),
        compiler_params=pltpu.CompilerParams(vmem_limit_bytes=16 * MIB),
        cost_estimate=cost(1e8, 4e5),
        name="weigh",
    )(points, factors)


def blend_kernel(left_ref, own_ref, right_ref, pieces_ref, out_ref):
    widened = jnp.concatenate([left_ref[...], own_ref[...], right_ref[...]], axis=0)
    out_ref[...] = lax.dot_general(
        pieces_ref[...],
        jnp.concatenate([widened, widened], axis=0),
        (((0,), (0,)), ((), ())),
        preferred_element_type=jnp.float32,
    ).astype(jnp.bfloat16)


def blend(left, own, right, pieces):
    return pl.pallas_call(
        blend_kernel,
        out_shape=jax.ShapeDtypeStruct((pieces.shape[1], own.shape[1]), jnp.bfloat16),
        compiler_params=pltpu.CompilerParams(vmem_limit_bytes=16 * MIB),
        cost_estimate=cost(1e9, 4e6),
        name="blend",
    )(left, own, right, pieces)


def center_kernel(*refs):
    *field_refs, deviation_ref, mean_ref = refs
    own = field_refs[0].shape[0]
    total = jnp.zeros(mean_ref.shape[1:], jnp.float32)
    for ref in field_refs:
        for k in range(own):
            total = total + ref[k].astype(jnp.float32)
    mean = total * (1.0 / ENSEMBLE_SIZE)
    mean_ref[0] = mean
    for s, ref in enumerate(field_refs):
        for k in range(own):
            deviation_ref[0, s * own + k] = (ref[k].astype(jnp.float32) - mean).astype(jnp.bfloat16)


def center(fields):
    own, quantities, columns = fields[0].shape
    blocks = columns // LANES
    block = lambda i: (0, 0, i)
    return pl.pallas_call(
        center_kernel,
        grid=(columns // LANES,),
        in_specs=[pl.BlockSpec((own, quantities, LANES), block)] * len(fields),
        out_specs=[
            pl.BlockSpec((1, ENSEMBLE_SIZE, quantities, LANES), lambda i: (i, 0, 0, 0)),
            pl.BlockSpec((1, quantities, LANES), lambda i: (i, 0, 0)),
        ],
        out_shape=[
            jax.ShapeDtypeStruct((blocks, ENSEMBLE_SIZE, quantities, LANES), jnp.bfloat16),
            jax.ShapeDtypeStruct((blocks, quantities, LANES), jnp.float32),
        ],
        compiler_params=pltpu.CompilerParams(vmem_limit_bytes=24 * MIB),
        cost_estimate=cost(1e9, 4e6),
        name="center",
    )(*fields)


def tip_kernel(weights_ref, out_ref):
    out_ref[0] = jnp.transpose(weights_ref[...].astype(jnp.float32))


def tip(weights):
    columns, entries = weights.shape
    return pl.pallas_call(
        tip_kernel,
        grid=(columns // LANES,),
        in_specs=[pl.BlockSpec((LANES, entries), lambda i: (i, 0))],
        out_specs=pl.BlockSpec((1, entries, LANES), lambda i: (i, 0, 0)),
        out_shape=jax.ShapeDtypeStruct((columns // LANES, entries, LANES), jnp.float32),
        compiler_params=pltpu.CompilerParams(vmem_limit_bytes=24 * MIB),
        cost_estimate=cost(1e9, 4e6),
        name="tip",
    )(weights)


def update_kernel(group_ref, weights_ref, deviation_ref, mean_ref, *out_refs, steps):
    own = out_refs[0].shape[0]
    groups = ENSEMBLE_SIZE // own
    for step, out_ref in zip(steps, out_refs):
        first = group_ref[step] * own
        for block in range(weights_ref.shape[0]):

            def body(pair, sums):
                sums = list(sums)
                for half in range(2):
                    s = 2 * pair + half
                    start = group_ref[s] * (own * ENSEMBLE_SIZE) + first
                    for k in range(own):
                        deviation = deviation_ref[block, s * own + k].astype(jnp.float32)
                        for j in range(own):
                            row = pl.ds(start + k * ENSEMBLE_SIZE + j, 1)
                            sums[j] = sums[j] + deviation * weights_ref[block, row, :]
                return tuple(sums)

            sums = lax.fori_loop(
                0, groups // 2, body, tuple(mean_ref[block] for _ in range(own))
            )
            for j in range(own):
                out_ref[j, :, block * LANES : (block + 1) * LANES] = sums[j].astype(jnp.bfloat16)


def update(group, steps, weights, deviation, mean):
    blocks, _, quantities, lanes = deviation.shape
    own = ENSEMBLE_SIZE // group.shape[0]
    whole = pl.BlockSpec(memory_space=pltpu.VMEM)
    return pl.pallas_call(
        functools.partial(update_kernel, steps=tuple(steps)),
        in_specs=[pl.BlockSpec(memory_space=pltpu.SMEM), whole, whole, whole],
        out_specs=[whole] * len(steps),
        out_shape=[jax.ShapeDtypeStruct((own, quantities, blocks * lanes), jnp.bfloat16)]
        * len(steps),
        compiler_params=pltpu.CompilerParams(vmem_limit_bytes=16 * MIB),
        cost_estimate=cost(3e9 * len(steps), 8e6),
        name="update",
    )(group, weights, deviation, mean)


def exchange(part, s, groups):
    if s == 0:
        return part
    return lax.ppermute(part, "member", [(i, i ^ s) for i in range(groups)])


def local_step(
    prior_ensemble, domain_site_mapping, neighbour_triples, stencil_factors, sparse_node_transforms
):
    own_members, quantities, cells = prior_ensemble.shape
    groups = lax.axis_size("member")
    patches = lax.axis_size("grid")
    columns = cells // groups
    per_source = columns // patches
    entries = ENSEMBLE_SIZE * ENSEMBLE_SIZE
    rows = own_members * quantities

    turned = turn(sparse_node_transforms)
    following = [(i, (i + 1) % patches) for i in range(patches)]
    preceding = [((i + 1) % patches, i) for i in range(patches)]
    left = lax.ppermute(turned[-RIM:], "grid", following)
    right = lax.ppermute(turned[:RIM], "grid", preceding)
    pieces = weigh(
        jnp.transpose(neighbour_triples, (1, 0, 2)),
        jnp.transpose(stencil_factors, (1, 0, 2)),
        turned.shape[0] + 2 * RIM,
    )
    blended = blend(left, turned, right, pieces)
    weights = lax.all_to_all(
        blended.reshape(patches, per_source, entries),
        "grid",
        split_axis=0,
        concat_axis=0,
        tiled=True,
    ).reshape(columns, entries)

    group = (lax.axis_index("member") ^ jnp.arange(groups, dtype=jnp.int32)).astype(jnp.int32)
    order = jnp.transpose(domain_site_mapping, (1, 0, 2)).reshape(groups, columns)[group]
    source_rows = prior_ensemble.reshape(rows, cells)
    steps = STEPS
    fields = [None] * groups
    for s in steps:
        chosen = pick_columns(source_rows, order[s : s + 1])
        fields[s] = exchange(chosen, s, groups).reshape(own_members, quantities, columns)
    deviation, mean = center(fields)
    spread = tip(weights)
    results = {}
    for first in range(0, groups, TOGETHER):
        now = steps[first : first + TOGETHER]
        parts = update(group, now, spread, deviation, mean)
        for s, part in zip(now, parts):
            results[s] = exchange(part.reshape(rows, columns), s, groups)
    positions = jnp.broadcast_to(order.reshape(cells, 1), (cells, LANES))
    placed = place_columns([results[s] for s in range(groups)], positions)
    return placed.reshape(own_members, quantities, cells)


def solution(mesh):
    return jax.shard_map(
        local_step,
        mesh=mesh,
        in_specs=(
            P("member", None, "grid"),
            P(None, None, "grid"),
            P("grid", None, "member"),
            P("grid", None, "member"),
            P(None, "grid"),
        ),
        out_specs=P("member", None, "grid"),
        check_vma=False,
    )
```

time: 128 us -> 134 us (1.047)
  waiting for transfers between devices: 29.9 us -> 43.4 us
  Pallas kernels: 45.6 us -> 39.9 us
  local copies, waits for them, and re-layouts: 9.68 us -> 7.51 us
    ppermute x14, waiting for transfers between devices: 28.1 us -> 43.2 us  [exchange(): return lax.ppermute(part, 'member', [(i, i ^ s) for i in range(groups)])]
    pallas_call x7, Pallas kernels: 31.4 us -> 28.1 us  [the longest x4 15.1 us: update(): pl.pallas_call(functools.partial(update_kernel, steps=tuple(steps)), in_s...]
    pallas_call x8, Pallas kernels: 11.8 us -> 9.72 us  [pick_columns(): pl.pallas_call(pick_kernel, out_shape=jax.ShapeDtypeStruct((rows, columns...]
    unnamed x21 -> x15, local copies, waits for them, and re-layouts: 7.68 us -> 6.13 us
    ppermute x1, waiting for transfers between devices: 1.81 us -> 0.27 us  [local_step(): left = lax.ppermute(turned[-RIM:], 'grid', following)]
  transfers between devices with their start and end apart: 17 -> 17, of which waited for: 4 -> 7; matrix products, arithmetic and copies ran while one was open for 1% -> 1% of each run, Pallas kernels for 18% -> 11%
where the time goes in v2:
time: 134 us; the launch traced here: 132 us
  waiting for transfers between devices  43.4 us (32%)
  starting transfers between devices  41.3 us (31%)
  Pallas kernels  39.9 us (30%)
  local copies, waits for them, and re-layouts  7.51 us (6%)
    ppermute x14, waiting for transfers between devices, exchange(): return lax.ppermute(part, 'member', [(i, i ^ s) for i in range(groups)])  43.2 us
    ppermute x14, starting transfers between devices, exchange(): return lax.ppermute(part, 'member', [(i, i ^ s) for i in range(groups)])  23.2 us
    pallas_call x4, Pallas kernels, update(): pl.pallas_call(functools.partial(update_kernel, steps=tuple(steps)), in_s...  15.1 us
    all_to_all x1, starting transfers between devices, local_step(): lax.all_to_all(blended.reshape(patches, per_source, entries), 'grid', spl...  14.8 us
    pallas_call x1, Pallas kernels, place_columns(): pl.pallas_call(place_kernel, grid=(cells // block,), in_specs=[whole] * (...  10.4 us
    pallas_call x8, Pallas kernels, pick_columns(): pl.pallas_call(pick_kernel, out_shape=jax.ShapeDtypeStruct((rows, columns...  9.72 us
    unnamed x15, local copies, waits for them, and re-layouts  6.13 us
    ppermute x1, starting transfers between devices, local_step(): right = lax.ppermute(turned[:RIM], 'grid', preceding)  3.24 us
  transfers between devices with their start and end apart: 17, of which 7 were waited for; matrix products, arithmetic and copies ran while one was open for 1% of the time, Pallas kernels for 11%

profile of v2, /device:TPU:30, one launch (start us, length us, event | category | flops | bytes accessed | tf_op | source)
XLA Modules:
  0.0 132.5 jit_solution(13250613010177079289)
XLA Ops:
  0.0 1.1 copy-done
  1.1 0.2 turn.1.own_ref
  1.4 0.1 collective-permute-start
  1.5 3.2 %collective-permute-start.1 = (bf16[16,1600]{1,0:T(8,128)(2,1)S(1)}, bf16[16,1600]{1,0:T(8,128)(2,1)S(1)}, u32[]{:S(2)}, u32[]{:S(2)}) collective-permute-start(bf16[16,1600]{1,0:T(8,128)(2,1)S(1)} %get-tuple-element.25), channel_id=1, source_target_pairs={{1,0},{2,1},{3,2},{4,3},{5,4},{6,5},{7,6},{8,7},{9,8},{10,9},{11,1... | collective-permute-start | bytes 153608 | tf_op jit(solution)/shard_map/ppermute | solution.py:257
  4.7 0.7 copy-done.2
  5.4 0.7 copy-done.3
  6.1 0.2 weigh.1.pieces_ref
  6.2 0.3 collective-permute-done.left_ref
  6.5 0.0 collective-permute-done.1.right_ref
  6.5 2.4 %blend.1 = bf16[512,1600]{1,0:T(8,128)(2,1)} custom-call(bf16[16,1600]{1,0:T(8,128)(2,1)S(1)} %collective-permute-done.left_ref, bf16[128,1600]{1,0:T(8,128)(2,1)S(1)} %turn.1.own_ref, bf16[16,1600]{1,0:T(8,128)(2,1)S(1)} %collective-permute-done.1.right_ref, bf16[320,512]{1,0:T(8,128)(2,1)S(1)} %weigh.1.pieces_ref), custom_call_target="tpu_custom_call" | custom-call | flops 1000000000 | bytes 4000000 | tf_op jit(solution)/shard_map/blend/pallas_call | solution.py:131
  8.9 14.8 %all-to-all-start = ((bf16[32,16,1600]{2,1,0:T(8,128)(2,1)}), bf16[32,16,1600]{2,1,0:T(8,128)(2,1)S(1)}, u32[]{:S(2)}, u32[]{:S(2)}) async-start(bf16[32,16,1600]{2,1,0:T(8,128)(2,1)} %bitcast.2), calls=%async_computation | async-start | bytes 3407872 | tf_op jit(solution)/shard_map/all_to_all | solution.py:264
  23.7 0.1 copy.7
  23.8 0.1 reshape.84
  23.9 0.6 gather_fusion
  24.5 0.0 copy-start.1
  24.5 1.5 %copy-done.1 = bf16[5,48,4096]{2,1,0:T(8,128)(2,1)S(1)} copy-done((bf16[5,48,4096]{2,1,0:T(8,128)(2,1)S(1)}, bf16[5,48,4096]{2,1,0:T(8,128)(2,1)}, u32[]{:S(2)}) %copy-start.1) | copy-done | bytes 1966104
  26.1 1.2 pick.11
  27.3 0.6 collective-permute-start.4
  27.8 1.2 pick.12
  29.1 0.1 collective-permute-start.5
  29.2 1.2 pick.13
  30.4 2.4 %collective-permute-start.6 = (bf16[240,512]{1,0:T(8,128)(2,1)S(1)}, bf16[240,512]{1,0:T(8,128)(2,1)S(1)}, u32[]{:S(2)}, u32[]{:S(2)}) collective-permute-start(bf16[240,512]{1,0:T(8,128)(2,1)S(1)} %pick.13), channel_id=1, source_target_pairs={{0,160},{32,128},{64,224},{96,192},{128,32},{160,0},{192,96},{224,... | collective-permute-start | bytes 737288 | tf_op jit(solution)/shard_map/ppermute | solution.py:239
  32.8 1.2 pick.14
  34.0 2.9 %collective-permute-start.7 = (bf16[240,512]{1,0:T(8,128)(2,1)S(1)}, bf16[240,512]{1,0:T(8,128)(2,1)S(1)}, u32[]{:S(2)}, u32[]{:S(2)}) collective-permute-start(bf16[240,512]{1,0:T(8,128)(2,1)S(1)} %pick.14), channel_id=1, source_target_pairs={{0,192},{32,224},{64,128},{96,160},{128,64},{160,96},{192,0},{224,... | collective-permute-start | bytes 737288 | tf_op jit(solution)/shard_map/ppermute | solution.py:239
  36.9 1.2 pick.15
  38.1 2.2 %collective-permute-start.8 = (bf16[240,512]{1,0:T(8,128)(2,1)S(1)}, bf16[240,512]{1,0:T(8,128)(2,1)S(1)}, u32[]{:S(2)}, u32[]{:S(2)}) collective-permute-start(bf16[240,512]{1,0:T(8,128)(2,1)S(1)} %pick.15), channel_id=1, source_target_pairs={{0,224},{32,192},{64,160},{96,128},{128,96},{160,64},{192,32},{224... | collective-permute-start | bytes 737288 | tf_op jit(solution)/shard_map/ppermute | solution.py:239
  40.3 1.2 pick.9
  41.5 1.2 pick.10
  42.8 0.0 collective-permute-done.4
  42.8 0.1 collective-permute-start.2
  42.9 24.2 %collective-permute-done.5 = bf16[240,512]{1,0:T(8,128)(2,1)S(1)} collective-permute-done((bf16[240,512]{1,0:T(8,128)(2,1)S(1)}, bf16[240,512]{1,0:T(8,128)(2,1)S(1)}, u32[]{:S(2)}, u32[]{:S(2)}) %collective-permute-start.5) | collective-permute-done | bytes 245792 | tf_op jit(solution)/shard_map/ppermute | solution.py:239
  67.1 1.5 %collective-permute-start.3 = (bf16[240,512]{1,0:T(8,128)(2,1)S(1)}, bf16[240,512]{1,0:T(8,128)(2,1)S(1)}, u32[]{:S(2)}, u32[]{:S(2)}) collective-permute-start(bf16[240,512]{1,0:T(8,128)(2,1)S(1)} %pick.10), channel_id=1, source_target_pairs={{0,64},{32,96},{64,0},{96,32},{128,192},{160,224},{192,128},{224,1... | collective-permute-start | bytes 737288 | tf_op jit(solution)/shard_map/ppermute | solution.py:239
  68.6 1.2 pick.8
  69.8 0.0 collective-permute-done.6
  69.8 0.0 collective-permute-done.7
  69.9 0.0 collective-permute-done.8
  69.9 0.0 collective-permute-done.2
  69.9 6.5 %collective-permute-done.3 = bf16[240,512]{1,0:T(8,128)(2,1)S(1)} collective-permute-done((bf16[240,512]{1,0:T(8,128)(2,1)S(1)}, bf16[240,512]{1,0:T(8,128)(2,1)S(1)}, u32[]{:S(2)}, u32[]{:S(2)}) %collective-permute-start.3) | collective-permute-done | bytes 245792 | tf_op jit(solution)/shard_map/ppermute | solution.py:239
  76.4 1.1 center.1
  77.6 0.0 copy-start.4
  77.6 1.3 copy-done.4
  78.8 0.0 all-to-all-done
  78.9 0.8 tip.1.weights_ref
  79.6 0.8 copy-done.5
  80.4 3.8 %update.7 = (bf16[5,48,512]{2,1,0:T(8,128)(2,1)S(1)}, bf16[5,48,512]{2,1,0:T(8,128)(2,1)S(1)}) custom-call(s32[8]{0:T(128)S(1)} %iota_xor_fusion.group_ref, f32[4,1600,128]{2,1,0:T(8,128)S(1)} %tip.1.weights_ref, bf16[4,40,48,128]{3,2,1,0:T(8,128)(2,1)S(1)} %copy-done.5, f32[4,48,128]{2,1,0:T(8,128)S(1)} %get-tuple-element.16.mean_ref), custom_call_target="tpu_custom_call" | custom-call | flops 6000000000 | bytes 8000000 | tf_op jit(solution)/shard_map/update/pallas_call | solution.py:224
  84.2 3.8 %update.6 = (bf16[5,48,512]{2,1,0:T(8,128)(2,1)S(1)}, bf16[5,48,512]{2,1,0:T(8,128)(2,1)S(1)}) custom-call(s32[8]{0:T(128)S(1)} %iota_xor_fusion.group_ref, f32[4,1600,128]{2,1,0:T(8,128)S(1)} %tip.1.weights_ref, bf16[4,40,48,128]{3,2,1,0:T(8,128)(2,1)S(1)} %copy-done.5, f32[4,48,128]{2,1,0:T(8,128)S(1)} %get-tuple-element.16.mean_ref), custom_call_target="tpu_custom_call" | custom-call | flops 6000000000 | bytes 8000000 | tf_op jit(solution)/shard_map/update/pallas_call | solution.py:224
  88.0 3.8 %update.5 = (bf16[5,48,512]{2,1,0:T(8,128)(2,1)S(1)}, bf16[5,48,512]{2,1,0:T(8,128)(2,1)S(1)}) custom-call(s32[8]{0:T(128)S(1)} %iota_xor_fusion.group_ref, f32[4,1600,128]{2,1,0:T(8,128)S(1)} %tip.1.weights_ref, bf16[4,40,48,128]{3,2,1,0:T(8,128)(2,1)S(1)} %copy-done.5, f32[4,48,128]{2,1,0:T(8,128)S(1)} %get-tuple-element.16.mean_ref), custom_call_target="tpu_custom_call" | custom-call | flops 6000000000 | bytes 8000000 | tf_op jit(solution)/shard_map/update/pallas_call | solution.py:224
  91.8 2.4 %collective-permute-start.14 = (bf16[240,512]{1,0:T(8,128)(2,1)S(1)}, bf16[240,512]{1,0:T(8,128)(2,1)S(1)}, u32[]{:S(2)}, u32[]{:S(2)}) collective-permute-start(bf16[240,512]{1,0:T(8,128)(2,1)S(1)} %bitcast.48), channel_id=1, source_target_pairs={{0,192},{32,224},{64,128},{96,160},{128,64},{160,96},{192,0},{224,... | collective-permute-start | bytes 737288 | tf_op jit(solution)/shard_map/ppermute | solution.py:239
  94.2 2.0 %collective-permute-start.15 = (bf16[240,512]{1,0:T(8,128)(2,1)S(1)}, bf16[240,512]{1,0:T(8,128)(2,1)S(1)}, u32[]{:S(2)}, u32[]{:S(2)}) collective-permute-start(bf16[240,512]{1,0:T(8,128)(2,1)S(1)} %bitcast.46), channel_id=1, source_target_pairs={{0,224},{32,192},{64,160},{96,128},{128,96},{160,64},{192,32},{224... | collective-permute-start | bytes 737288 | tf_op jit(solution)/shard_map/ppermute | solution.py:239
  96.2 3.8 %update.4 = (bf16[5,48,512]{2,1,0:T(8,128)(2,1)S(1)}, bf16[5,48,512]{2,1,0:T(8,128)(2,1)S(1)}) custom-call(s32[8]{0:T(128)S(1)} %iota_xor_fusion.group_ref, f32[4,1600,128]{2,1,0:T(8,128)S(1)} %tip.1.weights_ref, bf16[4,40,48,128]{3,2,1,0:T(8,128)(2,1)S(1)} %copy-done.5, f32[4,48,128]{2,1,0:T(8,128)S(1)} %get-tuple-element.16.mean_ref), custom_call_target="tpu_custom_call" | custom-call | flops 6000000000 | bytes 8000000 | tf_op jit(solution)/shard_map/update/pallas_call | solution.py:224
  100.0 1.2 collective-permute-start.12
  101.3 0.3 collective-permute-start.13
  101.6 2.2 %collective-permute-start.10 = (bf16[240,512]{1,0:T(8,128)(2,1)S(1)}, bf16[240,512]{1,0:T(8,128)(2,1)S(1)}, u32[]{:S(2)}, u32[]{:S(2)}) collective-permute-start(bf16[240,512]{1,0:T(8,128)(2,1)S(1)} %bitcast.41), channel_id=1, source_target_pairs={{0,64},{32,96},{64,0},{96,32},{128,192},{160,224},{192,128},{224,1... | collective-permute-start | bytes 737288 | tf_op jit(solution)/shard_map/ppermute | solution.py:239
  103.8 0.0 collective-permute-done.14.refs_6_
  103.8 2.5 %collective-permute-start.11 = (bf16[240,512]{1,0:T(8,128)(2,1)S(1)}, bf16[240,512]{1,0:T(8,128)(2,1)S(1)}, u32[]{:S(2)}, u32[]{:S(2)}) collective-permute-start(bf16[240,512]{1,0:T(8,128)(2,1)S(1)} %bitcast.39), channel_id=1, source_target_pairs={{0,96},{32,64},{64,32},{96,0},{128,224},{160,192},{192,160},{224,1... | collective-permute-start | bytes 737288 | tf_op jit(solution)/shard_map/ppermute | solution.py:239
  106.3 3.0 %collective-permute-done.15.refs_7_ = bf16[240,512]{1,0:T(8,128)(2,1)S(1)} collective-permute-done((bf16[240,512]{1,0:T(8,128)(2,1)S(1)}, bf16[240,512]{1,0:T(8,128)(2,1)S(1)}, u32[]{:S(2)}, u32[]{:S(2)}) %collective-permute-start.15) | collective-permute-done | bytes 245792 | tf_op jit(solution)/shard_map/ppermute | solution.py:239
  109.3 2.7 %collective-permute-start.9 = (bf16[240,512]{1,0:T(8,128)(2,1)S(1)}, bf16[240,512]{1,0:T(8,128)(2,1)S(1)}, u32[]{:S(2)}, u32[]{:S(2)}) collective-permute-start(bf16[240,512]{1,0:T(8,128)(2,1)S(1)} %bitcast.43), channel_id=1, source_target_pairs={{0,32},{32,0},{64,96},{96,64},{128,160},{160,128},{192,224},{224,1... | collective-permute-start | bytes 737288 | tf_op jit(solution)/shard_map/ppermute | solution.py:239
  112.1 5.0 %collective-permute-done.12.refs_4_ = bf16[240,512]{1,0:T(8,128)(2,1)S(1)} collective-permute-done((bf16[240,512]{1,0:T(8,128)(2,1)S(1)}, bf16[240,512]{1,0:T(8,128)(2,1)S(1)}, u32[]{:S(2)}, u32[]{:S(2)}) %collective-permute-start.12) | collective-permute-done | bytes 245792 | tf_op jit(solution)/shard_map/ppermute | solution.py:239
  117.0 0.0 collective-permute-done.13.refs_5_
  117.0 1.8 %collective-permute-done.10.refs_2_ = bf16[240,512]{1,0:T(8,128)(2,1)S(1)} collective-permute-done((bf16[240,512]{1,0:T(8,128)(2,1)S(1)}, bf16[240,512]{1,0:T(8,128)(2,1)S(1)}, u32[]{:S(2)}, u32[]{:S(2)}) %collective-permute-start.10) | collective-permute-done | bytes 245792 | tf_op jit(solution)/shard_map/ppermute | solution.py:239
  118.8 0.0 collective-permute-done.11.refs_3_
  118.8 2.6 %collective-permute-done.9.refs_1_ = bf16[240,512]{1,0:T(8,128)(2,1)S(1)} collective-permute-done((bf16[240,512]{1,0:T(8,128)(2,1)S(1)}, bf16[240,512]{1,0:T(8,128)(2,1)S(1)}, u32[]{:S(2)}, u32[]{:S(2)}) %collective-permute-start.9) | collective-permute-done | bytes 245792 | tf_op jit(solution)/shard_map/ppermute | solution.py:239
  121.4 0.6 broadcast_in_dim.9.refs_8_
  122.0 10.4 %place.1 = bf16[240,4096]{1,0:T(8,128)(2,1)} custom-call(bf16[240,512]{1,0:T(8,128)(2,1)S(1)} %bitcast.52, bf16[240,512]{1,0:T(8,128)(2,1)S(1)} %collective-permute-done.9.refs_1_, bf16[240,512]{1,0:T(8,128)(2,1)S(1)} %collective-permute-done.10.refs_2_, bf16[240,512]{1,0:T(8,128)(2,1)S(1)} %collective-permute-done.11.refs_3_, ...), custom_call_target="tpu_custom_call" | custom-call | flops 8053063680 | bytes 3932160 | tf_op jit(solution)/shard_map/place/pallas_call | solution.py:69
  (12 shorter events, 0.1 us)
Async XLA Ops:
  0.0 1.1 copy-start
  1.4 5.1 %collective-permute-start = (bf16[16,1600]{1,0:T(8,128)(2,1)S(1)}, bf16[16,1600]{1,0:T(8,128)(2,1)S(1)}, u32[]{:S(2)}, u32[]{:S(2)}) collective-permute-start(bf16[16,1600]{1,0:T(8,128)(2,1)S(1)} %get-tuple-element.26), channel_id=1, source_target_pairs={{0,1},{1,2},{2,3},{3,4},{4,5},{5,6},{6,7},{7,8},{8,9},{9,10},{10,1... | collective-permute-start | bytes 153608 | tf_op jit(solution)/shard_map/ppermute | solution.py:256
  1.5 5.1 %collective-permute-start.1 = (bf16[16,1600]{1,0:T(8,128)(2,1)S(1)}, bf16[16,1600]{1,0:T(8,128)(2,1)S(1)}, u32[]{:S(2)}, u32[]{:S(2)}) collective-permute-start(bf16[16,1600]{1,0:T(8,128)(2,1)S(1)} %get-tuple-element.25), channel_id=1, source_target_pairs={{1,0},{2,1},{3,2},{4,3},{5,4},{6,5},{7,6},{8,7},{9,8},{10,9},{11,1... | collective-permute-start | bytes 153608 | tf_op jit(solution)/shard_map/ppermute | solution.py:257
  4.7 0.7 copy-start.2
  5.4 0.7 copy-start.3
  8.9 14.8 %copy-start.6 = (s32[32,8,16]{0,2,1:T(8,128)S(1)}, s32[32,8,16]{0,2,1:T(8,128)}, u32[]{:S(2)}) copy-start(s32[32,8,16]{0,2,1:T(8,128)} %param.6) | copy-start | bytes 49156
  8.9 70.0 %all-to-all-start = ((bf16[32,16,1600]{2,1,0:T(8,128)(2,1)}), bf16[32,16,1600]{2,1,0:T(8,128)(2,1)S(1)}, u32[]{:S(2)}, u32[]{:S(2)}) async-start(bf16[32,16,1600]{2,1,0:T(8,128)(2,1)} %bitcast.2), calls=%async_computation | async-start | bytes 3407872 | tf_op jit(solution)/shard_map/all_to_all | solution.py:264
  24.5 1.5 %copy-start.1 = (bf16[5,48,4096]{2,1,0:T(8,128)(2,1)S(1)}, bf16[5,48,4096]{2,1,0:T(8,128)(2,1)}, u32[]{:S(2)}) copy-start(bf16[5,48,4096]{2,1,0:T(8,128)(2,1)} %param.5) | copy-start | bytes 5898244
  27.3 15.5 %collective-permute-start.4 = (bf16[240,512]{1,0:T(8,128)(2,1)S(1)}, bf16[240,512]{1,0:T(8,128)(2,1)S(1)}, u32[]{:S(2)}, u32[]{:S(2)}) collective-permute-start(bf16[240,512]{1,0:T(8,128)(2,1)S(1)} %pick.11), channel_id=1, source_target_pairs={{0,96},{32,64},{64,32},{96,0},{128,224},{160,192},{192,160},{224,1... | collective-permute-start | bytes 737288 | tf_op jit(solution)/shard_map/ppermute | solution.py:239
  29.1 38.0 %collective-permute-start.5 = (bf16[240,512]{1,0:T(8,128)(2,1)S(1)}, bf16[240,512]{1,0:T(8,128)(2,1)S(1)}, u32[]{:S(2)}, u32[]{:S(2)}) collective-permute-start(bf16[240,512]{1,0:T(8,128)(2,1)S(1)} %pick.12), channel_id=1, source_target_pairs={{0,128},{32,160},{64,192},{96,224},{128,0},{160,32},{192,64},{224,... | collective-permute-start | bytes 737288 | tf_op jit(solution)/shard_map/ppermute | solution.py:239
  30.4 39.4 %collective-permute-start.6 = (bf16[240,512]{1,0:T(8,128)(2,1)S(1)}, bf16[240,512]{1,0:T(8,128)(2,1)S(1)}, u32[]{:S(2)}, u32[]{:S(2)}) collective-permute-start(bf16[240,512]{1,0:T(8,128)(2,1)S(1)} %pick.13), channel_id=1, source_target_pairs={{0,160},{32,128},{64,224},{96,192},{128,32},{160,0},{192,96},{224,... | collective-permute-start | bytes 737288 | tf_op jit(solution)/shard_map/ppermute | solution.py:239
  34.0 35.8 %collective-permute-start.7 = (bf16[240,512]{1,0:T(8,128)(2,1)S(1)}, bf16[240,512]{1,0:T(8,128)(2,1)S(1)}, u32[]{:S(2)}, u32[]{:S(2)}) collective-permute-start(bf16[240,512]{1,0:T(8,128)(2,1)S(1)} %pick.14), channel_id=1, source_target_pairs={{0,192},{32,224},{64,128},{96,160},{128,64},{160,96},{192,0},{224,... | collective-permute-start | bytes 737288 | tf_op jit(solution)/shard_map/ppermute | solution.py:239
  38.1 31.7 %collective-permute-start.8 = (bf16[240,512]{1,0:T(8,128)(2,1)S(1)}, bf16[240,512]{1,0:T(8,128)(2,1)S(1)}, u32[]{:S(2)}, u32[]{:S(2)}) collective-permute-start(bf16[240,512]{1,0:T(8,128)(2,1)S(1)} %pick.15), channel_id=1, source_target_pairs={{0,224},{32,192},{64,160},{96,128},{128,96},{160,64},{192,32},{224... | collective-permute-start | bytes 737288 | tf_op jit(solution)/shard_map/ppermute | solution.py:239
  42.8 27.1 %collective-permute-start.2 = (bf16[240,512]{1,0:T(8,128)(2,1)S(1)}, bf16[240,512]{1,0:T(8,128)(2,1)S(1)}, u32[]{:S(2)}, u32[]{:S(2)}) collective-permute-start(bf16[240,512]{1,0:T(8,128)(2,1)S(1)} %pick.9), channel_id=1, source_target_pairs={{0,32},{32,0},{64,96},{96,64},{128,160},{160,128},{192,224},{224,1... | collective-permute-start | bytes 737288 | tf_op jit(solution)/shard_map/ppermute | solution.py:239
  67.1 9.3 %collective-permute-start.3 = (bf16[240,512]{1,0:T(8,128)(2,1)S(1)}, bf16[240,512]{1,0:T(8,128)(2,1)S(1)}, u32[]{:S(2)}, u32[]{:S(2)}) collective-permute-start(bf16[240,512]{1,0:T(8,128)(2,1)S(1)} %pick.10), channel_id=1, source_target_pairs={{0,64},{32,96},{64,0},{96,32},{128,192},{160,224},{192,128},{224,1... | collective-permute-start | bytes 737288 | tf_op jit(solution)/shard_map/ppermute | solution.py:239
  77.6 1.3 copy-start.4
  78.8 1.5 %copy-start.5 = (bf16[4,40,48,128]{3,2,1,0:T(8,128)(2,1)S(1)}, bf16[4,40,48,128]{3,2,1,0:T(8,128)(2,1)}, u32[]{:S(2)}) copy-start(bf16[4,40,48,128]{3,2,1,0:T(8,128)(2,1)} %copy-done.4) | copy-start | bytes 5898244
  91.8 12.0 %collective-permute-start.14 = (bf16[240,512]{1,0:T(8,128)(2,1)S(1)}, bf16[240,512]{1,0:T(8,128)(2,1)S(1)}, u32[]{:S(2)}, u32[]{:S(2)}) collective-permute-start(bf16[240,512]{1,0:T(8,128)(2,1)S(1)} %bitcast.48), channel_id=1, source_target_pairs={{0,192},{32,224},{64,128},{96,160},{128,64},{160,96},{192,0},{224,... | collective-permute-start | bytes 737288 | tf_op jit(solution)/shard_map/ppermute | solution.py:239
  94.2 15.1 %collective-permute-start.15 = (bf16[240,512]{1,0:T(8,128)(2,1)S(1)}, bf16[240,512]{1,0:T(8,128)(2,1)S(1)}, u32[]{:S(2)}, u32[]{:S(2)}) collective-permute-start(bf16[240,512]{1,0:T(8,128)(2,1)S(1)} %bitcast.46), channel_id=1, source_target_pairs={{0,224},{32,192},{64,160},{96,128},{128,96},{160,64},{192,32},{224... | collective-permute-start | bytes 737288 | tf_op jit(solution)/shard_map/ppermute | solution.py:239
  100.0 17.0 %collective-permute-start.12 = (bf16[240,512]{1,0:T(8,128)(2,1)S(1)}, bf16[240,512]{1,0:T(8,128)(2,1)S(1)}, u32[]{:S(2)}, u32[]{:S(2)}) collective-permute-start(bf16[240,512]{1,0:T(8,128)(2,1)S(1)} %bitcast.45), channel_id=1, source_target_pairs={{0,128},{32,160},{64,192},{96,224},{128,0},{160,32},{192,64},{224,... | collective-permute-start | bytes 737288 | tf_op jit(solution)/shard_map/ppermute | solution.py:239
  101.3 15.8 %collective-permute-start.13 = (bf16[240,512]{1,0:T(8,128)(2,1)S(1)}, bf16[240,512]{1,0:T(8,128)(2,1)S(1)}, u32[]{:S(2)}, u32[]{:S(2)}) collective-permute-start(bf16[240,512]{1,0:T(8,128)(2,1)S(1)} %bitcast.42), channel_id=1, source_target_pairs={{0,160},{32,128},{64,224},{96,192},{128,32},{160,0},{192,96},{224,... | collective-permute-start | bytes 737288 | tf_op jit(solution)/shard_map/ppermute | solution.py:239
  101.6 17.2 %collective-permute-start.10 = (bf16[240,512]{1,0:T(8,128)(2,1)S(1)}, bf16[240,512]{1,0:T(8,128)(2,1)S(1)}, u32[]{:S(2)}, u32[]{:S(2)}) collective-permute-start(bf16[240,512]{1,0:T(8,128)(2,1)S(1)} %bitcast.41), channel_id=1, source_target_pairs={{0,64},{32,96},{64,0},{96,32},{128,192},{160,224},{192,128},{224,1... | collective-permute-start | bytes 737288 | tf_op jit(solution)/shard_map/ppermute | solution.py:239
  103.8 15.0 %collective-permute-start.11 = (bf16[240,512]{1,0:T(8,128)(2,1)S(1)}, bf16[240,512]{1,0:T(8,128)(2,1)S(1)}, u32[]{:S(2)}, u32[]{:S(2)}) collective-permute-start(bf16[240,512]{1,0:T(8,128)(2,1)S(1)} %bitcast.39), channel_id=1, source_target_pairs={{0,96},{32,64},{64,32},{96,0},{128,224},{160,192},{192,160},{224,1... | collective-permute-start | bytes 737288 | tf_op jit(solution)/shard_map/ppermute | solution.py:239
  109.3 12.1 %collective-permute-start.9 = (bf16[240,512]{1,0:T(8,128)(2,1)S(1)}, bf16[240,512]{1,0:T(8,128)(2,1)S(1)}, u32[]{:S(2)}, u32[]{:S(2)}) collective-permute-start(bf16[240,512]{1,0:T(8,128)(2,1)S(1)} %bitcast.43), channel_id=1, source_target_pairs={{0,32},{32,0},{64,96},{96,64},{128,160},{160,128},{192,224},{224,1... | collective-permute-start | bytes 737288 | tf_op jit(solution)/shard_map/ppermute | solution.py:239

commit v3 on v2

--- a/solution.py
+++ b/solution.py
@@ -14,6 +14,7 @@
 MIB = 1024 * 1024
 STEPS = [6, 7, 5, 4, 2, 3, 1, 0]
 TOGETHER = 2
+PLACED = [[6, 7, 0], [5, 4, 2, 3, 1]]
 
 
 def cost(flops, moved):
@@ -22,28 +23,34 @@
 
 def pick_kernel(rows_ref, targets_ref, out_ref):
     cells = rows_ref.shape[1]
-    columns = targets_ref.shape[1]
-    cell_ids = lax.broadcasted_iota(jnp.int32, (cells, columns), 0)
-    onehot = jnp.where(cell_ids == targets_ref[...], 1.0, 0.0).astype(jnp.bfloat16)
-    out_ref[...] = jnp.dot(
+    cell_ids = lax.broadcasted_iota(jnp.int32, (cells, targets_ref.shape[2]), 0)
+    onehot = jnp.where(cell_ids == targets_ref[0], 1.0, 0.0).astype(jnp.bfloat16)
+    out_ref[0] = jnp.dot(
         rows_ref[...], onehot, preferred_element_type=jnp.float32
     ).astype(jnp.bfloat16)
 
 
 def pick_columns(source_rows, targets):
     rows, cells = source_rows.shape
-    columns = targets.shape[1]
+    count, _, columns = targets.shape
     return pl.pallas_call(
         pick_kernel,
-        out_shape=jax.ShapeDtypeStruct((rows, columns), jnp.bfloat16),
+        grid=(count,),
+        in_specs=[
+            pl.BlockSpec(memory_space=pltpu.VMEM),
+            pl.BlockSpec((1, 1, columns), lambda i: (i, 0, 0)),
+        ],
+        out_specs=pl.BlockSpec((1, rows, columns), lambda i: (i, 0, 0)),
+        out_shape=jax.ShapeDtypeStruct((count, rows, columns), jnp.bfloat16),
         compiler_params=pltpu.CompilerParams(vmem_limit_bytes=24 * MIB),
-        cost_estimate=cost(2 * rows * cells * columns, 2 * rows * columns),
+        cost_estimate=cost(2 * count * rows * cells * columns, 2 * count * rows * columns),
         name="pick",
     )(source_rows, targets)
 
 
-def place_kernel(*refs):
-    *part_refs, positions_ref, out_ref, rows_ref = refs
+def place_kernel(*refs, count, more):
+    part_refs, positions_ref = refs[:count], refs[count]
+    out_ref, rows_ref = refs[-2:]
     columns = part_refs[0].shape[1]
     block = out_ref.shape[1]
     step = pl.program_id(0)
@@ -56,27 +63,29 @@
     wide = jnp.concatenate([positions_ref[...]] * (block // LANES), axis=1)
     target_ids = step * block + lax.broadcasted_iota(jnp.int32, wide.shape, 1)
     onehot = jnp.where(wide == target_ids, 1.0, 0.0).astype(jnp.bfloat16)
-    out_ref[...] = jnp.dot(
-        rows_ref[...], onehot, preferred_element_type=jnp.float32
-    ).astype(jnp.bfloat16)
-
-
-def place_columns(parts, positions):
+    placed = jnp.dot(rows_ref[...], onehot, preferred_element_type=jnp.float32)
+    if more:
+        placed = placed + refs[count + 1][...].astype(jnp.float32)
+    out_ref[...] = placed.astype(jnp.bfloat16)
+
+
+def place_columns(parts, positions, before, cells):
     rows, columns = parts[0].shape
-    cells = columns * len(parts)
     block = 512
     whole = pl.BlockSpec(memory_space=pltpu.VMEM)
-    return pl.pallas_call(
-        place_kernel,
+    block_spec = pl.BlockSpec((rows, block), lambda i: (0, i))
+    more = before is not None
+    return pl.pallas_call(
+        functools.partial(place_kernel, count=len(parts), more=more),
         grid=(cells // block,),
-        in_specs=[whole] * (len(parts) + 1),
-        out_specs=pl.BlockSpec((rows, block), lambda i: (0, i)),
+        in_specs=[whole] * (len(parts) + 1) + [block_spec] * more,
+        out_specs=block_spec,
         out_shape=jax.ShapeDtypeStruct((rows, cells), jnp.bfloat16),
-        scratch_shapes=[pltpu.VMEM((rows, cells), jnp.bfloat16)],
-        compiler_params=pltpu.CompilerParams(vmem_limit_bytes=24 * MIB),
-        cost_estimate=cost(2 * rows * cells * cells, 4 * rows * cells),
+        scratch_shapes=[pltpu.VMEM((rows, columns * len(parts)), jnp.bfloat16)],
+        compiler_params=pltpu.CompilerParams(vmem_limit_bytes=20 * MIB),
+        cost_estimate=cost(2 * rows * cells * columns * len(parts), 4 * rows * cells),
         name="place",
-    )(*parts, positions)
+    )(*parts, positions, *([before] if more else []))
 
 
 def turn_kernel(transforms_ref, out_ref):
@@ -273,10 +282,19 @@
     order = jnp.transpose(domain_site_mapping, (1, 0, 2)).reshape(groups, columns)[group]
     source_rows = prior_ensemble.reshape(rows, cells)
     steps = STEPS
+    half = groups // 2
+    targets = order.reshape(groups, 1, columns)
+    crossing = pick_columns(source_rows, targets[half:])
+    arrived = exchange(crossing, half, groups)
     fields = [None] * groups
-    for s in steps:
-        chosen = pick_columns(source_rows, order[s : s + 1])
-        fields[s] = exchange(chosen, s, groups).reshape(own_members, quantities, columns)
+    fields[half] = arrived[0]
+    for s in range(1, half):
+        chosen = pick_columns(source_rows, targets[s : s + 1])
+        fields[s] = exchange(chosen[0], s, groups)
+    fields[0] = pick_columns(source_rows, targets[:1])[0]
+    for s in range(1, half):
+        fields[half + s] = exchange(arrived[s], s, groups)
+    fields = [part.reshape(own_members, quantities, columns) for part in fields]
     deviation, mean = center(fields)
     spread = tip(weights)
     results = {}
@@ -285,8 +303,11 @@
         parts = update(group, now, spread, deviation, mean)
         for s, part in zip(now, parts):
             results[s] = exchange(part.reshape(rows, columns), s, groups)
-    positions = jnp.broadcast_to(order.reshape(cells, 1), (cells, LANES))
-    placed = place_columns([results[s] for s in range(groups)], positions)
+    placed = None
+    for now in PLACED:
+        positions = jnp.concatenate([order[s] for s in now]).reshape(-1, 1)
+        positions = jnp.broadcast_to(positions, (positions.shape[0], LANES))
+        placed = place_columns([results[s] for s in now], positions, placed, cells)
     return placed.reshape(own_members, quantities, cells)
 
 

time: 134 us -> 139 us (1.037)
  Pallas kernels: 39.9 us -> 43.8 us
  local copies, waits for them, and re-layouts: 7.51 us -> 8.97 us
    pallas_call x9 -> x7, Pallas kernels: 20.2 us -> 24 us  [the longest x2 12.1 us: place_columns(): pl.pallas_call(functools.partial(place_kernel, count=len(parts), more=mor...]
    unnamed x15 -> x20, local copies, waits for them, and re-layouts: 6.13 us -> 6.14 us
  transfers between devices with their start and end apart: 17 -> 17, of which waited for: 7 -> 9; matrix products, arithmetic and copies ran while one was open for 1% -> 2% of each run, Pallas kernels for 11% -> 16%
where the time goes in v3:
time: 139 us; the launch traced here: 137 us
  Pallas kernels  43.8 us (32%)
  waiting for transfers between devices  42.7 us (31%)
  starting transfers between devices  41.1 us (30%)
  local copies, waits for them, and re-layouts  8.97 us (6%)
    ppermute x14, waiting for transfers between devices, exchange(): return lax.ppermute(part, 'member', [(i, i ^ s) for i in range(groups)])  42.5 us
    ppermute x14, starting transfers between devices, exchange(): return lax.ppermute(part, 'member', [(i, i ^ s) for i in range(groups)])  23 us
    pallas_call x4, Pallas kernels, update(): pl.pallas_call(functools.partial(update_kernel, steps=tuple(steps)), in_s...  15.1 us
    all_to_all x1, starting transfers between devices, local_step(): lax.all_to_all(blended.reshape(patches, per_source, entries), 'grid', spl...  14.8 us
    pallas_call x2, Pallas kernels, place_columns(): pl.pallas_call(functools.partial(place_kernel, count=len(parts), more=mor...  12.1 us
    pallas_call x5, Pallas kernels, pick_columns(): pl.pallas_call(pick_kernel, grid=(count,), in_specs=[pl.BlockSpec(memory_...  11.9 us
    unnamed x20, local copies, waits for them, and re-layouts  6.14 us
    ppermute x1, starting transfers between devices, local_step(): right = lax.ppermute(turned[:RIM], 'grid', preceding)  3.24 us
  transfers between devices with their start and end apart: 17, of which 9 were waited for; matrix products, arithmetic and copies ran while one was open for 2% of the time, Pallas kernels for 16%

profile of v3, /device:TPU:30, one launch (start us, length us, event | category | flops | bytes accessed | tf_op | source)
XLA Modules:
  0.0 136.9 jit_solution(10274331787273408526)
XLA Ops:
  0.0 1.1 copy-done
  1.1 0.2 turn.1.own_ref
  1.4 0.1 collective-permute-start
  1.5 3.2 %collective-permute-start.1 = (bf16[16,1600]{1,0:T(8,128)(2,1)S(1)}, bf16[16,1600]{1,0:T(8,128)(2,1)S(1)}, u32[]{:S(2)}, u32[]{:S(2)}) collective-permute-start(bf16[16,1600]{1,0:T(8,128)(2,1)S(1)} %get-tuple-element.29), channel_id=1, source_target_pairs={{1,0},{2,1},{3,2},{4,3},{5,4},{6,5},{7,6},{8,7},{9,8},{10,9},{11,1... | collective-permute-start | bytes 153608 | tf_op jit(solution)/shard_map/ppermute | solution.py:266
  4.7 0.7 copy-done.3
  5.4 0.7 copy-done.4
  6.1 0.2 weigh.1.pieces_ref
  6.2 0.3 collective-permute-done.left_ref
  6.5 0.0 collective-permute-done.1.right_ref
  6.5 2.4 %blend.1 = bf16[512,1600]{1,0:T(8,128)(2,1)} custom-call(bf16[16,1600]{1,0:T(8,128)(2,1)S(1)} %collective-permute-done.left_ref, bf16[128,1600]{1,0:T(8,128)(2,1)S(1)} %turn.1.own_ref, bf16[16,1600]{1,0:T(8,128)(2,1)S(1)} %collective-permute-done.1.right_ref, bf16[320,512]{1,0:T(8,128)(2,1)S(1)} %weigh.1.pieces_ref), custom_call_target="tpu_custom_call" | custom-call | flops 1000000000 | bytes 4000000 | tf_op jit(solution)/shard_map/blend/pallas_call | solution.py:140
  8.9 14.8 %all-to-all-start = ((bf16[32,16,1600]{2,1,0:T(8,128)(2,1)}), bf16[32,16,1600]{2,1,0:T(8,128)(2,1)S(1)}, u32[]{:S(2)}, u32[]{:S(2)}) async-start(bf16[32,16,1600]{2,1,0:T(8,128)(2,1)} %bitcast.2), calls=%async_computation | async-start | bytes 3407872 | tf_op jit(solution)/shard_map/all_to_all | solution.py:273
  23.7 0.1 copy.7
  23.8 0.1 reshape.86
  23.9 0.6 gather_fusion
  24.5 0.0 copy-start.1
  24.5 1.5 %copy-done.1 = bf16[5,48,4096]{2,1,0:T(8,128)(2,1)S(1)} copy-done((bf16[5,48,4096]{2,1,0:T(8,128)(2,1)S(1)}, bf16[5,48,4096]{2,1,0:T(8,128)(2,1)}, u32[]{:S(2)}) %copy-start.1) | copy-done | bytes 1966104
  26.1 4.9 %pick.9 = bf16[4,240,512]{2,1,0:T(8,128)(2,1)S(1)} custom-call(bf16[240,4096]{1,0:T(8,128)(2,1)S(1)} %bitcast.52, s32[4,1,512]{2,1,0:T(1,128)S(1)} %slice.75.targets_ref), custom_call_target="tpu_custom_call" | custom-call | flops 4026531840 | bytes 983040 | tf_op jit(solution)/shard_map/pick/pallas_call | solution.py:36
  31.0 0.1 collective-permute-start.5
  31.1 1.9 %pick.6 = bf16[1,240,512]{2,1,0:T(8,128)(2,1)} custom-call(bf16[240,4096]{1,0:T(8,128)(2,1)S(1)} %bitcast.53, s32[1,1,512]{2,1,0:T(1,128)S(1)} %get-tuple-element.33.targets_ref), custom_call_target="tpu_custom_call" | custom-call | flops 1006632960 | bytes 245760 | tf_op jit(solution)/shard_map/pick/pallas_call | solution.py:36
  33.0 0.8 collective-permute-start.2
  33.8 1.9 %pick.7 = bf16[1,240,512]{2,1,0:T(8,128)(2,1)} custom-call(bf16[240,4096]{1,0:T(8,128)(2,1)S(1)} %bitcast.54, s32[1,1,512]{2,1,0:T(1,128)S(1)} %get-tuple-element.34.targets_ref), custom_call_target="tpu_custom_call" | custom-call | flops 1006632960 | bytes 245760 | tf_op jit(solution)/shard_map/pick/pallas_call | solution.py:36
  35.8 1.1 collective-permute-start.3
  36.9 1.9 %pick.8 = bf16[1,240,512]{2,1,0:T(8,128)(2,1)} custom-call(bf16[240,4096]{1,0:T(8,128)(2,1)S(1)} %bitcast.55, s32[1,1,512]{2,1,0:T(1,128)S(1)} %get-tuple-element.35.targets_ref), custom_call_target="tpu_custom_call" | custom-call | flops 1006632960 | bytes 245760 | tf_op jit(solution)/shard_map/pick/pallas_call | solution.py:36
  38.8 2.8 %collective-permute-start.4 = (bf16[240,512]{1,0:T(8,128)(2,1)}, bf16[240,512]{1,0:T(8,128)(2,1)S(1)}, u32[]{:S(2)}, u32[]{:S(2)}) collective-permute-start(bf16[240,512]{1,0:T(8,128)(2,1)} %bitcast.16), channel_id=1, source_target_pairs={{0,96},{32,64},{64,32},{96,0},{128,224},{160,192},{192,160},{224,1... | collective-permute-start | bytes 737288 | tf_op jit(solution)/shard_map/ppermute | solution.py:248
  41.6 26.2 %collective-permute-done.5 = bf16[4,240,512]{2,1,0:T(8,128)(2,1)} collective-permute-done((bf16[4,240,512]{2,1,0:T(8,128)(2,1)S(1)}, bf16[4,240,512]{2,1,0:T(8,128)(2,1)}, u32[]{:S(2)}, u32[]{:S(2)}) %collective-permute-start.5) | collective-permute-done | bytes 983072 | tf_op jit(solution)/shard_map/ppermute | solution.py:248
  67.8 1.4 %slice_bitcast_fusion = (bf16[240,512]{1,0:T(8,128)(2,1)S(1)}, bf16[240,512]{1,0:T(8,128)(2,1)S(1)}, bf16[240,512]{1,0:T(8,128)(2,1)S(1)}, bf16[1,240,512]{2,1,0:T(8,128)(2,1)S(1)}) fusion(bf16[4,240,512]{2,1,0:T(8,128)(2,1)} %collective-permute-done.5), kind=kLoop, calls=%fused_computation.1 | loop fusion | bytes 1966080 | tf_op jit(solution)/shard_map/squeeze | solution.py:296
  69.2 0.9 collective-permute-start.6
  70.1 1.1 collective-permute-start.7
  71.2 0.0 collective-permute-done.2
  71.2 2.8 %collective-permute-start.8 = (bf16[240,512]{1,0:T(8,128)(2,1)S(1)}, bf16[240,512]{1,0:T(8,128)(2,1)S(1)}, u32[]{:S(2)}, u32[]{:S(2)}) collective-permute-start(bf16[240,512]{1,0:T(8,128)(2,1)S(1)} %get-tuple-element.25), channel_id=1, source_target_pairs={{0,96},{32,64},{64,32},{96,0},{128,224},{160,192},{192,160},{224,1... | collective-permute-start | bytes 737288 | tf_op jit(solution)/shard_map/ppermute | solution.py:248
  74.0 1.2 pick.5
  75.2 0.0 collective-permute-done.3
  75.2 0.0 collective-permute-done.4
  75.2 2.9 %collective-permute-done.6 = bf16[240,512]{1,0:T(8,128)(2,1)S(1)} collective-permute-done((bf16[240,512]{1,0:T(8,128)(2,1)S(1)}, bf16[240,512]{1,0:T(8,128)(2,1)S(1)}, u32[]{:S(2)}, u32[]{:S(2)}) %collective-permute-start.6) | collective-permute-done | bytes 245792 | tf_op jit(solution)/shard_map/ppermute | solution.py:248
  78.1 3.7 %collective-permute-done.7 = bf16[240,512]{1,0:T(8,128)(2,1)S(1)} collective-permute-done((bf16[240,512]{1,0:T(8,128)(2,1)S(1)}, bf16[240,512]{1,0:T(8,128)(2,1)S(1)}, u32[]{:S(2)}, u32[]{:S(2)}) %collective-permute-start.7) | collective-permute-done | bytes 245792 | tf_op jit(solution)/shard_map/ppermute | solution.py:248
  81.8 2.6 %collective-permute-done.8 = bf16[240,512]{1,0:T(8,128)(2,1)S(1)} collective-permute-done((bf16[240,512]{1,0:T(8,128)(2,1)S(1)}, bf16[240,512]{1,0:T(8,128)(2,1)S(1)}, u32[]{:S(2)}, u32[]{:S(2)}) %collective-permute-start.8) | collective-permute-done | bytes 245792 | tf_op jit(solution)/shard_map/ppermute | solution.py:248
  84.4 1.1 center.1
  85.5 0.0 copy-start.5
  85.6 1.3 copy-done.5
  86.8 0.0 all-to-all-done
  86.8 0.8 tip.1.weights_ref
  87.6 0.8 copy-done.6
  88.4 3.8 %update.4 = (bf16[5,48,512]{2,1,0:T(8,128)(2,1)S(1)}, bf16[5,48,512]{2,1,0:T(8,128)(2,1)S(1)}) custom-call(s32[8]{0:T(128)S(1)} %iota_xor_fusion.group_ref, f32[4,1600,128]{2,1,0:T(8,128)S(1)} %tip.1.weights_ref, bf16[4,40,48,128]{3,2,1,0:T(8,128)(2,1)S(1)} %copy-done.6, f32[4,48,128]{2,1,0:T(8,128)S(1)} %get-tuple-element.16.mean_ref), custom_call_target="tpu_custom_call" | custom-call | flops 6000000000 | bytes 8000000 | tf_op jit(solution)/shard_map/update/pallas_call | solution.py:233
  92.2 3.8 %update.5 = (bf16[5,48,512]{2,1,0:T(8,128)(2,1)S(1)}, bf16[5,48,512]{2,1,0:T(8,128)(2,1)S(1)}) custom-call(s32[8]{0:T(128)S(1)} %iota_xor_fusion.group_ref, f32[4,1600,128]{2,1,0:T(8,128)S(1)} %tip.1.weights_ref, bf16[4,40,48,128]{3,2,1,0:T(8,128)(2,1)S(1)} %copy-done.6, f32[4,48,128]{2,1,0:T(8,128)S(1)} %get-tuple-element.16.mean_ref), custom_call_target="tpu_custom_call" | custom-call | flops 6000000000 | bytes 8000000 | tf_op jit(solution)/shard_map/update/pallas_call | solution.py:233
  96.0 3.8 %update.7 = (bf16[5,48,512]{2,1,0:T(8,128)(2,1)S(1)}, bf16[5,48,512]{2,1,0:T(8,128)(2,1)S(1)}) custom-call(s32[8]{0:T(128)S(1)} %iota_xor_fusion.group_ref, f32[4,1600,128]{2,1,0:T(8,128)S(1)} %tip.1.weights_ref, bf16[4,40,48,128]{3,2,1,0:T(8,128)(2,1)S(1)} %copy-done.6, f32[4,48,128]{2,1,0:T(8,128)S(1)} %get-tuple-element.16.mean_ref), custom_call_target="tpu_custom_call" | custom-call | flops 6000000000 | bytes 8000000 | tf_op jit(solution)/shard_map/update/pallas_call | solution.py:233
  99.8 2.9 %collective-permute-start.14 = (bf16[240,512]{1,0:T(8,128)(2,1)S(1)}, bf16[240,512]{1,0:T(8,128)(2,1)S(1)}, u32[]{:S(2)}, u32[]{:S(2)}) collective-permute-start(bf16[240,512]{1,0:T(8,128)(2,1)S(1)} %bitcast.69), channel_id=1, source_target_pairs={{0,192},{32,224},{64,128},{96,160},{128,64},{160,96},{192,0},{224,... | collective-permute-start | bytes 737288 | tf_op jit(solution)/shard_map/ppermute | solution.py:248
  102.7 1.6 %collective-permute-start.15 = (bf16[240,512]{1,0:T(8,128)(2,1)S(1)}, bf16[240,512]{1,0:T(8,128)(2,1)S(1)}, u32[]{:S(2)}, u32[]{:S(2)}) collective-permute-start(bf16[240,512]{1,0:T(8,128)(2,1)S(1)} %bitcast.68), channel_id=1, source_target_pairs={{0,224},{32,192},{64,160},{96,128},{128,96},{160,64},{192,32},{224... | collective-permute-start | bytes 737288 | tf_op jit(solution)/shard_map/ppermute | solution.py:248
  104.3 3.8 %update.6 = (bf16[5,48,512]{2,1,0:T(8,128)(2,1)S(1)}, bf16[5,48,512]{2,1,0:T(8,128)(2,1)S(1)}) custom-call(s32[8]{0:T(128)S(1)} %iota_xor_fusion.group_ref, f32[4,1600,128]{2,1,0:T(8,128)S(1)} %tip.1.weights_ref, bf16[4,40,48,128]{3,2,1,0:T(8,128)(2,1)S(1)} %copy-done.6, f32[4,48,128]{2,1,0:T(8,128)S(1)} %get-tuple-element.16.mean_ref), custom_call_target="tpu_custom_call" | custom-call | flops 6000000000 | bytes 8000000 | tf_op jit(solution)/shard_map/update/pallas_call | solution.py:233
  108.1 1.6 %collective-permute-start.9 = (bf16[240,512]{1,0:T(8,128)(2,1)S(1)}, bf16[240,512]{1,0:T(8,128)(2,1)S(1)}, u32[]{:S(2)}, u32[]{:S(2)}) collective-permute-start(bf16[240,512]{1,0:T(8,128)(2,1)S(1)} %bitcast.63), channel_id=1, source_target_pairs={{0,160},{32,128},{64,224},{96,192},{128,32},{160,0},{192,96},{224,... | collective-permute-start | bytes 737288 | tf_op jit(solution)/shard_map/ppermute | solution.py:248
  109.7 0.7 collective-permute-start.10
  110.4 2.2 %collective-permute-start.11 = (bf16[240,512]{1,0:T(8,128)(2,1)S(1)}, bf16[240,512]{1,0:T(8,128)(2,1)S(1)}, u32[]{:S(2)}, u32[]{:S(2)}) collective-permute-start(bf16[240,512]{1,0:T(8,128)(2,1)S(1)} %bitcast.61), channel_id=1, source_target_pairs={{0,64},{32,96},{64,0},{96,32},{128,192},{160,224},{192,128},{224,1... | collective-permute-start | bytes 737288 | tf_op jit(solution)/shard_map/ppermute | solution.py:248
  112.6 0.0 collective-permute-done.14.refs_0_
  112.6 1.8 %collective-permute-start.12 = (bf16[240,512]{1,0:T(8,128)(2,1)S(1)}, bf16[240,512]{1,0:T(8,128)(2,1)S(1)}, u32[]{:S(2)}, u32[]{:S(2)}) collective-permute-start(bf16[240,512]{1,0:T(8,128)(2,1)S(1)} %bitcast.60), channel_id=1, source_target_pairs={{0,96},{32,64},{64,32},{96,0},{128,224},{160,192},{192,160},{224,1... | collective-permute-start | bytes 737288 | tf_op jit(solution)/shard_map/ppermute | solution.py:248
  114.4 2.6 %collective-permute-done.15.refs_1_ = bf16[240,512]{1,0:T(8,128)(2,1)S(1)} collective-permute-done((bf16[240,512]{1,0:T(8,128)(2,1)S(1)}, bf16[240,512]{1,0:T(8,128)(2,1)S(1)}, u32[]{:S(2)}, u32[]{:S(2)}) %collective-permute-start.15) | collective-permute-done | bytes 245792 | tf_op jit(solution)/shard_map/ppermute | solution.py:248
  117.0 2.5 %collective-permute-start.13 = (bf16[240,512]{1,0:T(8,128)(2,1)S(1)}, bf16[240,512]{1,0:T(8,128)(2,1)S(1)}, u32[]{:S(2)}, u32[]{:S(2)}) collective-permute-start(bf16[240,512]{1,0:T(8,128)(2,1)S(1)} %bitcast.64), channel_id=1, source_target_pairs={{0,32},{32,0},{64,96},{96,64},{128,160},{160,128},{192,224},{224,1... | collective-permute-start | bytes 737288 | tf_op jit(solution)/shard_map/ppermute | solution.py:248
  119.6 0.3 broadcast_in_dim.5.refs_3_
  119.8 4.6 %place.2.refs_6_ = bf16[240,4096]{1,0:T(8,128)(2,1)S(1)} custom-call(bf16[240,512]{1,0:T(8,128)(2,1)S(1)} %collective-permute-done.14.refs_0_, bf16[240,512]{1,0:T(8,128)(2,1)S(1)} %collective-permute-done.15.refs_1_, bf16[240,512]{1,0:T(8,128)(2,1)S(1)} %bitcast.72, s32[1536,128]{1,0:T(8,128)S(1)} %broadcast_in_dim.5.refs_3_), custom_call_target="tpu_custom_call" | custom-call | flops 3019898880 | bytes 3932160 | tf_op jit(solution)/shard_map/place/pallas_call | solution.py:78
  124.5 0.0 collective-permute-done.9.refs_0_
  124.5 0.0 collective-permute-done.10.refs_1_
  124.5 2.2 %collective-permute-done.11.refs_2_ = bf16[240,512]{1,0:T(8,128)(2,1)S(1)} collective-permute-done((bf16[240,512]{1,0:T(8,128)(2,1)S(1)}, bf16[240,512]{1,0:T(8,128)(2,1)S(1)}, u32[]{:S(2)}, u32[]{:S(2)}) %collective-permute-start.11) | collective-permute-done | bytes 245792 | tf_op jit(solution)/shard_map/ppermute | solution.py:248
  126.6 0.4 collective-permute-done.12.refs_3_
  127.0 1.9 %collective-permute-done.13.refs_4_ = bf16[240,512]{1,0:T(8,128)(2,1)S(1)} collective-permute-done((bf16[240,512]{1,0:T(8,128)(2,1)S(1)}, bf16[240,512]{1,0:T(8,128)(2,1)S(1)}, u32[]{:S(2)}, u32[]{:S(2)}) %collective-permute-start.13) | collective-permute-done | bytes 245792 | tf_op jit(solution)/shard_map/ppermute | solution.py:248
  128.9 0.4 broadcast_in_dim.4.refs_5_
  129.3 7.5 %place.3 = bf16[240,4096]{1,0:T(8,128)(2,1)} custom-call(bf16[240,512]{1,0:T(8,128)(2,1)S(1)} %collective-permute-done.9.refs_0_, bf16[240,512]{1,0:T(8,128)(2,1)S(1)} %collective-permute-done.10.refs_1_, bf16[240,512]{1,0:T(8,128)(2,1)S(1)} %collective-permute-done.11.refs_2_, bf16[240,512]{1,0:T(8,128)(2,1)S(1)} %collective-permute-done.12.refs_3_, ...), custom_call_target="tpu_custom_call" | custom-call | flops 5033164800 | bytes 3932160 | tf_op jit(solution)/shard_map/place/pallas_call | solution.py:78
  (22 shorter events, 0.1 us)
Async XLA Ops:
  0.0 1.1 copy-start
  1.4 5.1 %collective-permute-start = (bf16[16,1600]{1,0:T(8,128)(2,1)S(1)}, bf16[16,1600]{1,0:T(8,128)(2,1)S(1)}, u32[]{:S(2)}, u32[]{:S(2)}) collective-permute-start(bf16[16,1600]{1,0:T(8,128)(2,1)S(1)} %get-tuple-element.30), channel_id=1, source_target_pairs={{0,1},{1,2},{2,3},{3,4},{4,5},{5,6},{6,7},{7,8},{8,9},{9,10},{10,1... | collective-permute-start | bytes 153608 | tf_op jit(solution)/shard_map/ppermute | solution.py:265
  1.5 5.1 %collective-permute-start.1 = (bf16[16,1600]{1,0:T(8,128)(2,1)S(1)}, bf16[16,1600]{1,0:T(8,128)(2,1)S(1)}, u32[]{:S(2)}, u32[]{:S(2)}) collective-permute-start(bf16[16,1600]{1,0:T(8,128)(2,1)S(1)} %get-tuple-element.29), channel_id=1, source_target_pairs={{1,0},{2,1},{3,2},{4,3},{5,4},{6,5},{7,6},{8,7},{9,8},{10,9},{11,1... | collective-permute-start | bytes 153608 | tf_op jit(solution)/shard_map/ppermute | solution.py:266
  4.7 0.7 copy-start.3
  5.4 0.7 copy-start.4
  8.9 14.8 %copy-start.7 = (s32[32,8,16]{0,2,1:T(8,128)S(1)}, s32[32,8,16]{0,2,1:T(8,128)}, u32[]{:S(2)}) copy-start(s32[32,8,16]{0,2,1:T(8,128)} %param.6) | copy-start | bytes 49156
  8.9 78.0 %all-to-all-start = ((bf16[32,16,1600]{2,1,0:T(8,128)(2,1)}), bf16[32,16,1600]{2,1,0:T(8,128)(2,1)S(1)}, u32[]{:S(2)}, u32[]{:S(2)}) async-start(bf16[32,16,1600]{2,1,0:T(8,128)(2,1)} %bitcast.2), calls=%async_computation | async-start | bytes 3407872 | tf_op jit(solution)/shard_map/all_to_all | solution.py:273
  24.5 1.5 %copy-start.1 = (bf16[5,48,4096]{2,1,0:T(8,128)(2,1)S(1)}, bf16[5,48,4096]{2,1,0:T(8,128)(2,1)}, u32[]{:S(2)}) copy-start(bf16[5,48,4096]{2,1,0:T(8,128)(2,1)} %param.5) | copy-start | bytes 5898244
  31.0 36.8 %collective-permute-start.5 = (bf16[4,240,512]{2,1,0:T(8,128)(2,1)S(1)}, bf16[4,240,512]{2,1,0:T(8,128)(2,1)}, u32[]{:S(2)}, u32[]{:S(2)}) collective-permute-start(bf16[4,240,512]{2,1,0:T(8,128)(2,1)S(1)} %pick.9), channel_id=1, source_target_pairs={{0,128},{32,160},{64,192},{96,224},{128,0},{160,32},{192,64},{224,... | collective-permute-start | bytes 2949128 | tf_op jit(solution)/shard_map/ppermute | solution.py:248
  33.0 38.2 %collective-permute-start.2 = (bf16[240,512]{1,0:T(8,128)(2,1)}, bf16[240,512]{1,0:T(8,128)(2,1)S(1)}, u32[]{:S(2)}, u32[]{:S(2)}) collective-permute-start(bf16[240,512]{1,0:T(8,128)(2,1)} %bitcast.10), channel_id=1, source_target_pairs={{0,32},{32,0},{64,96},{96,64},{128,160},{160,128},{192,224},{224,1... | collective-permute-start | bytes 737288 | tf_op jit(solution)/shard_map/ppermute | solution.py:248
  35.8 39.5 %collective-permute-start.3 = (bf16[240,512]{1,0:T(8,128)(2,1)}, bf16[240,512]{1,0:T(8,128)(2,1)S(1)}, u32[]{:S(2)}, u32[]{:S(2)}) collective-permute-start(bf16[240,512]{1,0:T(8,128)(2,1)} %bitcast.13), channel_id=1, source_target_pairs={{0,64},{32,96},{64,0},{96,32},{128,192},{160,224},{192,128},{224,1... | collective-permute-start | bytes 737288 | tf_op jit(solution)/shard_map/ppermute | solution.py:248
  38.8 36.5 %collective-permute-start.4 = (bf16[240,512]{1,0:T(8,128)(2,1)}, bf16[240,512]{1,0:T(8,128)(2,1)S(1)}, u32[]{:S(2)}, u32[]{:S(2)}) collective-permute-start(bf16[240,512]{1,0:T(8,128)(2,1)} %bitcast.16), channel_id=1, source_target_pairs={{0,96},{32,64},{64,32},{96,0},{128,224},{160,192},{192,160},{224,1... | collective-permute-start | bytes 737288 | tf_op jit(solution)/shard_map/ppermute | solution.py:248
  41.5 32.4 %copy-start.2 = (bf16[5,48,4096]{2,1,0:T(8,128)(2,1)S(1)}, bf16[5,48,4096]{2,1,0:T(8,128)(2,1)}, u32[]{:S(2)}) copy-start(bf16[5,48,4096]{2,1,0:T(8,128)(2,1)} %param.5) | copy-start | bytes 5898244
  69.2 8.9 %collective-permute-start.6 = (bf16[240,512]{1,0:T(8,128)(2,1)S(1)}, bf16[240,512]{1,0:T(8,128)(2,1)S(1)}, u32[]{:S(2)}, u32[]{:S(2)}) collective-permute-start(bf16[240,512]{1,0:T(8,128)(2,1)S(1)} %get-tuple-element.27), channel_id=1, source_target_pairs={{0,32},{32,0},{64,96},{96,64},{128,160},{160,128},{192,224},{224,1... | collective-permute-start | bytes 737288 | tf_op jit(solution)/shard_map/ppermute | solution.py:248
  70.1 11.7 %collective-permute-start.7 = (bf16[240,512]{1,0:T(8,128)(2,1)S(1)}, bf16[240,512]{1,0:T(8,128)(2,1)S(1)}, u32[]{:S(2)}, u32[]{:S(2)}) collective-permute-start(bf16[240,512]{1,0:T(8,128)(2,1)S(1)} %get-tuple-element.26), channel_id=1, source_target_pairs={{0,64},{32,96},{64,0},{96,32},{128,192},{160,224},{192,128},{224,1... | collective-permute-start | bytes 737288 | tf_op jit(solution)/shard_map/ppermute | solution.py:248
  71.2 13.2 %collective-permute-start.8 = (bf16[240,512]{1,0:T(8,128)(2,1)S(1)}, bf16[240,512]{1,0:T(8,128)(2,1)S(1)}, u32[]{:S(2)}, u32[]{:S(2)}) collective-permute-start(bf16[240,512]{1,0:T(8,128)(2,1)S(1)} %get-tuple-element.25), channel_id=1, source_target_pairs={{0,96},{32,64},{64,32},{96,0},{128,224},{160,192},{192,160},{224,1... | collective-permute-start | bytes 737288 | tf_op jit(solution)/shard_map/ppermute | solution.py:248
  85.5 1.3 copy-start.5
  86.8 1.5 %copy-start.6 = (bf16[4,40,48,128]{3,2,1,0:T(8,128)(2,1)S(1)}, bf16[4,40,48,128]{3,2,1,0:T(8,128)(2,1)}, u32[]{:S(2)}) copy-start(bf16[4,40,48,128]{3,2,1,0:T(8,128)(2,1)} %copy-done.5) | copy-start | bytes 5898244
  99.8 12.9 %collective-permute-start.14 = (bf16[240,512]{1,0:T(8,128)(2,1)S(1)}, bf16[240,512]{1,0:T(8,128)(2,1)S(1)}, u32[]{:S(2)}, u32[]{:S(2)}) collective-permute-start(bf16[240,512]{1,0:T(8,128)(2,1)S(1)} %bitcast.69), channel_id=1, source_target_pairs={{0,192},{32,224},{64,128},{96,160},{128,64},{160,96},{192,0},{224,... | collective-permute-start | bytes 737288 | tf_op jit(solution)/shard_map/ppermute | solution.py:248
  102.7 14.3 %collective-permute-start.15 = (bf16[240,512]{1,0:T(8,128)(2,1)S(1)}, bf16[240,512]{1,0:T(8,128)(2,1)S(1)}, u32[]{:S(2)}, u32[]{:S(2)}) collective-permute-start(bf16[240,512]{1,0:T(8,128)(2,1)S(1)} %bitcast.68), channel_id=1, source_target_pairs={{0,224},{32,192},{64,160},{96,128},{128,96},{160,64},{192,32},{224... | collective-permute-start | bytes 737288 | tf_op jit(solution)/shard_map/ppermute | solution.py:248
  108.1 16.3 %collective-permute-start.9 = (bf16[240,512]{1,0:T(8,128)(2,1)S(1)}, bf16[240,512]{1,0:T(8,128)(2,1)S(1)}, u32[]{:S(2)}, u32[]{:S(2)}) collective-permute-start(bf16[240,512]{1,0:T(8,128)(2,1)S(1)} %bitcast.63), channel_id=1, source_target_pairs={{0,160},{32,128},{64,224},{96,192},{128,32},{160,0},{192,96},{224,... | collective-permute-start | bytes 737288 | tf_op jit(solution)/shard_map/ppermute | solution.py:248
  109.7 14.7 %collective-permute-start.10 = (bf16[240,512]{1,0:T(8,128)(2,1)S(1)}, bf16[240,512]{1,0:T(8,128)(2,1)S(1)}, u32[]{:S(2)}, u32[]{:S(2)}) collective-permute-start(bf16[240,512]{1,0:T(8,128)(2,1)S(1)} %bitcast.62), channel_id=1, source_target_pairs={{0,128},{32,160},{64,192},{96,224},{128,0},{160,32},{192,64},{224,... | collective-permute-start | bytes 737288 | tf_op jit(solution)/shard_map/ppermute | solution.py:248
  110.4 16.2 %collective-permute-start.11 = (bf16[240,512]{1,0:T(8,128)(2,1)S(1)}, bf16[240,512]{1,0:T(8,128)(2,1)S(1)}, u32[]{:S(2)}, u32[]{:S(2)}) collective-permute-start(bf16[240,512]{1,0:T(8,128)(2,1)S(1)} %bitcast.61), channel_id=1, source_target_pairs={{0,64},{32,96},{64,0},{96,32},{128,192},{160,224},{192,128},{224,1... | collective-permute-start | bytes 737288 | tf_op jit(solution)/shard_map/ppermute | solution.py:248
  112.6 14.4 %collective-permute-start.12 = (bf16[240,512]{1,0:T(8,128)(2,1)S(1)}, bf16[240,512]{1,0:T(8,128)(2,1)S(1)}, u32[]{:S(2)}, u32[]{:S(2)}) collective-permute-start(bf16[240,512]{1,0:T(8,128)(2,1)S(1)} %bitcast.60), channel_id=1, source_target_pairs={{0,96},{32,64},{64,32},{96,0},{128,224},{160,192},{192,160},{224,1... | collective-permute-start | bytes 737288 | tf_op jit(solution)/shard_map/ppermute | solution.py:248
  117.0 11.9 %collective-permute-start.13 = (bf16[240,512]{1,0:T(8,128)(2,1)S(1)}, bf16[240,512]{1,0:T(8,128)(2,1)S(1)}, u32[]{:S(2)}, u32[]{:S(2)}) collective-permute-start(bf16[240,512]{1,0:T(8,128)(2,1)S(1)} %bitcast.64), channel_id=1, source_target_pairs={{0,32},{32,0},{64,96},{96,64},{128,160},{160,128},{192,224},{224,1... | collective-permute-start | bytes 737288 | tf_op jit(solution)/shard_map/ppermute | solution.py:248

commit v4 on v3

--- a/solution.py
+++ b/solution.py
@@ -14,7 +14,8 @@
 MIB = 1024 * 1024
 STEPS = [6, 7, 5, 4, 2, 3, 1, 0]
 TOGETHER = 2
-PLACED = [[6, 7, 0], [5, 4, 2, 3, 1]]
+BLEND = 256
+PLACED = [[6, 7, 5, 0], [4, 2, 3, 1]]
 
 
 def cost(flops, moved):
@@ -71,7 +72,7 @@
 
 def place_columns(parts, positions, before, cells):
     rows, columns = parts[0].shape
-    block = 512
+    block = 1024
     whole = pl.BlockSpec(memory_space=pltpu.VMEM)
     block_spec = pl.BlockSpec((rows, block), lambda i: (0, i))
     more = before is not None
@@ -82,25 +83,31 @@
         out_specs=block_spec,
         out_shape=jax.ShapeDtypeStruct((rows, cells), jnp.bfloat16),
         scratch_shapes=[pltpu.VMEM((rows, columns * len(parts)), jnp.bfloat16)],
-        compiler_params=pltpu.CompilerParams(vmem_limit_bytes=20 * MIB),
+        compiler_params=pltpu.CompilerParams(vmem_limit_bytes=32 * MIB),
         cost_estimate=cost(2 * rows * cells * columns * len(parts), 4 * rows * cells),
         name="place",
     )(*parts, positions, *([before] if more else []))
 
 
-def turn_kernel(transforms_ref, out_ref):
-    out_ref[...] = jnp.transpose(transforms_ref[...]).astype(jnp.bfloat16)
-
-
-def turn(transforms):
+def turn_kernel(transforms_ref, *refs):
+    head_ref, out_ref, tail_ref = refs[-3:]
+    turned = jnp.transpose(transforms_ref[...]).astype(jnp.bfloat16)
+    head_ref[...] = turned[:RIM]
+    out_ref[...] = turned
+    tail_ref[...] = turned[-RIM:]
+
+
+def turn(transforms, *before):
     entries, points = transforms.shape
     return pl.pallas_call(
         turn_kernel,
-        out_shape=jax.ShapeDtypeStruct((points, entries), jnp.bfloat16),
-        compiler_params=pltpu.CompilerParams(vmem_limit_bytes=24 * MIB),
-        cost_estimate=cost(1e8, 6 * entries * points),
+        out_shape=[
+            jax.ShapeDtypeStruct((count, entries), jnp.bfloat16) for count in (RIM, points, RIM)
+        ],
+        compiler_params=pltpu.CompilerParams(vmem_limit_bytes=12 * MIB),
+        cost_estimate=cost(2e9, 6 * entries * points),
         name="turn",
-    )(transforms)
+    )(transforms, *before)
 
 
 def weigh_kernel(points_ref, factors_ref, out_ref):
@@ -137,9 +144,15 @@
 
 
 def blend(left, own, right, pieces):
+    columns, entries = pieces.shape[1], own.shape[1]
+    block = BLEND
+    whole = pl.BlockSpec(memory_space=pltpu.VMEM)
     return pl.pallas_call(
         blend_kernel,
-        out_shape=jax.ShapeDtypeStruct((pieces.shape[1], own.shape[1]), jnp.bfloat16),
+        grid=(columns // block,),
+        in_specs=[whole, whole, whole, pl.BlockSpec((pieces.shape[0], block), lambda i: (0, i))],
+        out_specs=pl.BlockSpec((block, entries), lambda i: (i, 0)),
+        out_shape=jax.ShapeDtypeStruct((columns, entries), jnp.bfloat16),
         compiler_params=pltpu.CompilerParams(vmem_limit_bytes=16 * MIB),
         cost_estimate=cost(1e9, 4e6),
         name="blend",
@@ -259,11 +272,13 @@
     entries = ENSEMBLE_SIZE * ENSEMBLE_SIZE
     rows = own_members * quantities
 
-    turned = turn(sparse_node_transforms)
+    targets = jnp.transpose(domain_site_mapping, (1, 0, 2)).reshape(groups, 1, columns)
+    source_rows = prior_ensemble.reshape(rows, cells)
+    head, turned, tail = turn(sparse_node_transforms)
     following = [(i, (i + 1) % patches) for i in range(patches)]
     preceding = [((i + 1) % patches, i) for i in range(patches)]
-    left = lax.ppermute(turned[-RIM:], "grid", following)
-    right = lax.ppermute(turned[:RIM], "grid", preceding)
+    left = lax.ppermute(tail, "grid", following)
+    right = lax.ppermute(head, "grid", preceding)
     pieces = weigh(
         jnp.transpose(neighbour_triples, (1, 0, 2)),
         jnp.transpose(stencil_factors, (1, 0, 2)),
@@ -279,19 +294,21 @@
     ).reshape(columns, entries)
 
     group = (lax.axis_index("member") ^ jnp.arange(groups, dtype=jnp.int32)).astype(jnp.int32)
-    order = jnp.transpose(domain_site_mapping, (1, 0, 2)).reshape(groups, columns)[group]
-    source_rows = prior_ensemble.reshape(rows, cells)
+    order = targets.reshape(groups, columns)[group]
+    later = order.reshape(groups, 1, columns)
     steps = STEPS
     half = groups // 2
-    targets = order.reshape(groups, 1, columns)
-    crossing = pick_columns(source_rows, targets[half:])
+    crossing = pick_columns(source_rows, later[half + 2 :])
     arrived = exchange(crossing, half, groups)
+    crossing = pick_columns(source_rows, later[half : half + 2])
+    more = exchange(crossing, half, groups)
+    arrived = [more[0], more[1], arrived[0], arrived[1]]
     fields = [None] * groups
     fields[half] = arrived[0]
     for s in range(1, half):
-        chosen = pick_columns(source_rows, targets[s : s + 1])
+        chosen = pick_columns(source_rows, later[s : s + 1])
         fields[s] = exchange(chosen[0], s, groups)
-    fields[0] = pick_columns(source_rows, targets[:1])[0]
+    fields[0] = pick_columns(source_rows, later[:1])[0]
     for s in range(1, half):
         fields[half + s] = exchange(arrived[s], s, groups)
     fields = [part.reshape(own_members, quantities, columns) for part in fields]

time: 139 us -> 135 us (0.971)
  waiting for transfers between devices: 42.7 us -> 46.9 us
  Pallas kernels: 43.8 us -> 40.2 us
  local copies, waits for them, and re-layouts: 8.97 us -> 6.26 us
  starting transfers between devices: 41.1 us -> 39.1 us
    ppermute x14 -> x15, waiting for transfers between devices: 42.5 us -> 45.2 us  [exchange(): return lax.ppermute(part, 'member', [(i, i ^ s) for i in range(groups)])]
    pallas_call x5 -> x6, Pallas kernels: 11.9 us -> 9.77 us  [pick_columns(): pl.pallas_call(pick_kernel, grid=(count,), in_specs=[pl.BlockSpec(memory_...]
    ppermute x14 -> x15, starting transfers between devices: 23 us -> 21 us  [exchange(): return lax.ppermute(part, 'member', [(i, i ^ s) for i in range(groups)])]
    unnamed x20 -> x14, local copies, waits for them, and re-layouts: 6.14 us -> 4.75 us
  transfers between devices with their start and end apart: 17 -> 18, of which waited for: 9 -> 9; matrix products, arithmetic and copies ran while one was open for 2% -> 1% of each run, Pallas kernels for 16% -> 15%
where the time goes in v4:
time: 135 us; the launch traced here: 133 us
  waiting for transfers between devices  46.9 us (35%)
  Pallas kernels  40.2 us (30%)
  starting transfers between devices  39.1 us (29%)
  local copies, waits for them, and re-layouts  6.26 us (5%)
    ppermute x15, waiting for transfers between devices, exchange(): return lax.ppermute(part, 'member', [(i, i ^ s) for i in range(groups)])  45.2 us
    ppermute x15, starting transfers between devices, exchange(): return lax.ppermute(part, 'member', [(i, i ^ s) for i in range(groups)])  21 us
    pallas_call x4, Pallas kernels, update(): pl.pallas_call(functools.partial(update_kernel, steps=tuple(steps)), in_s...  15.1 us
    all_to_all x1, starting transfers between devices, local_step(): lax.all_to_all(blended.reshape(patches, per_source, entries), 'grid', spl...  14.8 us
    pallas_call x2, Pallas kernels, place_columns(): pl.pallas_call(functools.partial(place_kernel, count=len(parts), more=mor...  10.8 us
    pallas_call x6, Pallas kernels, pick_columns(): pl.pallas_call(pick_kernel, grid=(count,), in_specs=[pl.BlockSpec(memory_...  9.77 us
    unnamed x14, local copies, waits for them, and re-layouts  4.75 us
    ppermute x1, starting transfers between devices, local_step(): right = lax.ppermute(head, 'grid', preceding)  3.24 us
  transfers between devices with their start and end apart: 18, of which 9 were waited for; matrix products, arithmetic and copies ran while one was open for 1% of the time, Pallas kernels for 15%

profile of v4, /device:TPU:30, one launch (start us, length us, event | category | flops | bytes accessed | tf_op | source)
XLA Modules:
  0.0 132.8 jit_solution(2396814233759531886)
XLA Ops:
  0.0 1.1 copy-done.1
  1.1 0.2 turn.1
  1.4 0.1 collective-permute-start
  1.4 3.2 %collective-permute-start.1 = (bf16[16,1600]{1,0:T(8,128)(2,1)S(1)}, bf16[16,1600]{1,0:T(8,128)(2,1)S(1)}, u32[]{:S(2)}, u32[]{:S(2)}) collective-permute-start(bf16[16,1600]{1,0:T(8,128)(2,1)S(1)} %get-tuple-element.20), channel_id=1, source_target_pairs={{1,0},{2,1},{3,2},{4,3},{5,4},{6,5},{7,6},{8,7},{9,8},{10,9},{11,1... | collective-permute-start | bytes 153608 | tf_op jit(solution)/shard_map/ppermute | solution.py:281
  4.7 0.2 weigh.1.pieces_ref
  4.9 1.6 %collective-permute-done.left_ref = bf16[16,1600]{1,0:T(8,128)(2,1)S(1)} collective-permute-done((bf16[16,1600]{1,0:T(8,128)(2,1)S(1)}, bf16[16,1600]{1,0:T(8,128)(2,1)S(1)}, u32[]{:S(2)}, u32[]{:S(2)}) %collective-permute-start) | collective-permute-done | bytes 51232 | tf_op jit(solution)/shard_map/ppermute | solution.py:280
  6.5 0.0 collective-permute-done.1.right_ref
  6.5 2.3 %blend.1 = bf16[512,1600]{1,0:T(8,128)(2,1)} custom-call(bf16[16,1600]{1,0:T(8,128)(2,1)S(1)} %collective-permute-done.left_ref, bf16[128,1600]{1,0:T(8,128)(2,1)S(1)} %get-tuple-element.19.own_ref, bf16[16,1600]{1,0:T(8,128)(2,1)S(1)} %collective-permute-done.1.right_ref, bf16[320,512]{1,0:T(8,128)(2,1)S(1)} %weigh.1.pieces_ref), custom_call_target="tpu_custom_call" | custom-call | flops 1000000000 | bytes 4000000 | tf_op jit(solution)/shard_map/blend/pallas_call | solution.py:150
  8.8 14.8 %all-to-all-start = ((bf16[32,16,1600]{2,1,0:T(8,128)(2,1)}), bf16[32,16,1600]{2,1,0:T(8,128)(2,1)S(1)}, u32[]{:S(2)}, u32[]{:S(2)}) async-start(bf16[32,16,1600]{2,1,0:T(8,128)(2,1)} %bitcast.2), calls=%async_computation | async-start | bytes 3407872 | tf_op jit(solution)/shard_map/all_to_all | solution.py:288
  23.6 0.1 copy.7
  23.7 0.1 reshape_reshape.3
  23.8 0.6 gather_fusion
  24.4 0.0 copy-start
  24.4 1.5 %copy-done = bf16[5,48,4096]{2,1,0:T(8,128)(2,1)S(1)} copy-done((bf16[5,48,4096]{2,1,0:T(8,128)(2,1)S(1)}, bf16[5,48,4096]{2,1,0:T(8,128)(2,1)}, u32[]{:S(2)}) %copy-start) | copy-done | bytes 1966104
  26.0 2.5 %pick.10 = bf16[2,240,512]{2,1,0:T(8,128)(2,1)S(1)} custom-call(bf16[240,4096]{1,0:T(8,128)(2,1)S(1)} %bitcast.52, s32[2,1,512]{2,1,0:T(1,128)S(1)} %slice.73.targets_ref), custom_call_target="tpu_custom_call" | custom-call | flops 2013265920 | bytes 491520 | tf_op jit(solution)/shard_map/pick/pallas_call | solution.py:37
  28.4 0.1 collective-permute-start.5
  28.6 1.2 pick.7
  29.8 0.9 collective-permute-start.2
  30.7 2.5 %pick.11 = bf16[2,240,512]{2,1,0:T(8,128)(2,1)S(1)} custom-call(bf16[240,4096]{1,0:T(8,128)(2,1)S(1)} %bitcast.54, s32[2,1,512]{2,1,0:T(1,128)S(1)} %slice.77.targets_ref), custom_call_target="tpu_custom_call" | custom-call | flops 2013265920 | bytes 491520 | tf_op jit(solution)/shard_map/pick/pallas_call | solution.py:37
  33.2 2.1 %collective-permute-start.7 = (bf16[2,240,512]{2,1,0:T(8,128)(2,1)S(1)}, bf16[2,240,512]{2,1,0:T(8,128)(2,1)S(1)}, u32[]{:S(2)}, u32[]{:S(2)}) collective-permute-start(bf16[2,240,512]{2,1,0:T(8,128)(2,1)S(1)} %pick.11), channel_id=1, source_target_pairs={{0,128},{32,160},{64,192},{96,224},{128,0},{160,32},{192,64},{224,... | collective-permute-start | bytes 1474568 | tf_op jit(solution)/shard_map/ppermute | solution.py:261
  35.3 1.2 pick.8
  36.5 1.2 collective-permute-start.3
  37.7 1.2 pick.9
  38.9 2.8 %collective-permute-start.4 = (bf16[240,512]{1,0:T(8,128)(2,1)S(1)}, bf16[240,512]{1,0:T(8,128)(2,1)S(1)}, u32[]{:S(2)}, u32[]{:S(2)}) collective-permute-start(bf16[240,512]{1,0:T(8,128)(2,1)S(1)} %bitcast.66), channel_id=1, source_target_pairs={{0,96},{32,64},{64,32},{96,0},{128,224},{160,192},{192,160},{224,1... | collective-permute-start | bytes 737288 | tf_op jit(solution)/shard_map/ppermute | solution.py:261
  41.8 10.1 %collective-permute-done.5 = bf16[2,240,512]{2,1,0:T(8,128)(2,1)S(1)} collective-permute-done((bf16[2,240,512]{2,1,0:T(8,128)(2,1)S(1)}, bf16[2,240,512]{2,1,0:T(8,128)(2,1)S(1)}, u32[]{:S(2)}, u32[]{:S(2)}) %collective-permute-start.5) | collective-permute-done | bytes 491552 | tf_op jit(solution)/shard_map/ppermute | solution.py:261
  51.9 0.9 collective-permute-start.6
  52.9 14.1 %collective-permute-done.7 = bf16[2,240,512]{2,1,0:T(8,128)(2,1)S(1)} collective-permute-done((bf16[2,240,512]{2,1,0:T(8,128)(2,1)S(1)}, bf16[2,240,512]{2,1,0:T(8,128)(2,1)S(1)}, u32[]{:S(2)}, u32[]{:S(2)}) %collective-permute-start.7) | collective-permute-done | bytes 491552 | tf_op jit(solution)/shard_map/ppermute | solution.py:261
  66.9 1.5 %collective-permute-start.8 = (bf16[240,512]{1,0:T(8,128)(2,1)S(1)}, bf16[240,512]{1,0:T(8,128)(2,1)S(1)}, u32[]{:S(2)}, u32[]{:S(2)}) collective-permute-start(bf16[240,512]{1,0:T(8,128)(2,1)S(1)} %get-tuple-element.32), channel_id=1, source_target_pairs={{0,64},{32,96},{64,0},{96,32},{128,192},{160,224},{192,128},{224,1... | collective-permute-start | bytes 737288 | tf_op jit(solution)/shard_map/ppermute | solution.py:261
  68.4 0.0 collective-permute-done.2
  68.4 2.1 %collective-permute-start.9 = (bf16[240,512]{1,0:T(8,128)(2,1)S(1)}, bf16[240,512]{1,0:T(8,128)(2,1)S(1)}, u32[]{:S(2)}, u32[]{:S(2)}) collective-permute-start(bf16[240,512]{1,0:T(8,128)(2,1)S(1)} %get-tuple-element.31), channel_id=1, source_target_pairs={{0,96},{32,64},{64,32},{96,0},{128,224},{160,192},{192,160},{224,1... | collective-permute-start | bytes 737288 | tf_op jit(solution)/shard_map/ppermute | solution.py:261
  70.5 1.2 pick.6
  71.8 0.0 collective-permute-done.3
  71.8 0.0 collective-permute-done.4
  71.8 0.0 collective-permute-done.6
  71.8 4.6 %collective-permute-done.8 = bf16[240,512]{1,0:T(8,128)(2,1)S(1)} collective-permute-done((bf16[240,512]{1,0:T(8,128)(2,1)S(1)}, bf16[240,512]{1,0:T(8,128)(2,1)S(1)}, u32[]{:S(2)}, u32[]{:S(2)}) %collective-permute-start.8) | collective-permute-done | bytes 245792 | tf_op jit(solution)/shard_map/ppermute | solution.py:261
  76.4 5.2 %collective-permute-done.9 = bf16[240,512]{1,0:T(8,128)(2,1)S(1)} collective-permute-done((bf16[240,512]{1,0:T(8,128)(2,1)S(1)}, bf16[240,512]{1,0:T(8,128)(2,1)S(1)}, u32[]{:S(2)}, u32[]{:S(2)}) %collective-permute-start.9) | collective-permute-done | bytes 245792 | tf_op jit(solution)/shard_map/ppermute | solution.py:261
  81.6 1.1 center.1
  82.8 0.0 copy-start.4
  82.8 1.3 copy-done.4
  84.0 0.0 all-to-all-done
  84.0 0.8 tip.1.weights_ref
  84.8 0.8 copy-done.5
  85.6 3.8 %update.4 = (bf16[5,48,512]{2,1,0:T(8,128)(2,1)S(1)}, bf16[5,48,512]{2,1,0:T(8,128)(2,1)S(1)}) custom-call(s32[8]{0:T(128)S(1)} %iota_xor_fusion.group_ref, f32[4,1600,128]{2,1,0:T(8,128)S(1)} %tip.1.weights_ref, bf16[4,40,48,128]{3,2,1,0:T(8,128)(2,1)S(1)} %copy-done.5, f32[4,48,128]{2,1,0:T(8,128)S(1)} %get-tuple-element.22.mean_ref), custom_call_target="tpu_custom_call" | custom-call | flops 6000000000 | bytes 8000000 | tf_op jit(solution)/shard_map/update/pallas_call | solution.py:246
  89.4 3.8 %update.5 = (bf16[5,48,512]{2,1,0:T(8,128)(2,1)S(1)}, bf16[5,48,512]{2,1,0:T(8,128)(2,1)S(1)}) custom-call(s32[8]{0:T(128)S(1)} %iota_xor_fusion.group_ref, f32[4,1600,128]{2,1,0:T(8,128)S(1)} %tip.1.weights_ref, bf16[4,40,48,128]{3,2,1,0:T(8,128)(2,1)S(1)} %copy-done.5, f32[4,48,128]{2,1,0:T(8,128)S(1)} %get-tuple-element.22.mean_ref), custom_call_target="tpu_custom_call" | custom-call | flops 6000000000 | bytes 8000000 | tf_op jit(solution)/shard_map/update/pallas_call | solution.py:246
  93.2 3.8 %update.7 = (bf16[5,48,512]{2,1,0:T(8,128)(2,1)S(1)}, bf16[5,48,512]{2,1,0:T(8,128)(2,1)S(1)}) custom-call(s32[8]{0:T(128)S(1)} %iota_xor_fusion.group_ref, f32[4,1600,128]{2,1,0:T(8,128)S(1)} %tip.1.weights_ref, bf16[4,40,48,128]{3,2,1,0:T(8,128)(2,1)S(1)} %copy-done.5, f32[4,48,128]{2,1,0:T(8,128)S(1)} %get-tuple-element.22.mean_ref), custom_call_target="tpu_custom_call" | custom-call | flops 6000000000 | bytes 8000000 | tf_op jit(solution)/shard_map/update/pallas_call | solution.py:246
  97.0 2.1 %collective-permute-start.14 = (bf16[240,512]{1,0:T(8,128)(2,1)S(1)}, bf16[240,512]{1,0:T(8,128)(2,1)S(1)}, u32[]{:S(2)}, u32[]{:S(2)}) collective-permute-start(bf16[240,512]{1,0:T(8,128)(2,1)S(1)} %bitcast.73), channel_id=1, source_target_pairs={{0,192},{32,224},{64,128},{96,160},{128,64},{160,96},{192,0},{224,... | collective-permute-start | bytes 737288 | tf_op jit(solution)/shard_map/ppermute | solution.py:261
  99.1 1.5 %collective-permute-start.15 = (bf16[240,512]{1,0:T(8,128)(2,1)S(1)}, bf16[240,512]{1,0:T(8,128)(2,1)S(1)}, u32[]{:S(2)}, u32[]{:S(2)}) collective-permute-start(bf16[240,512]{1,0:T(8,128)(2,1)S(1)} %bitcast.72), channel_id=1, source_target_pairs={{0,224},{32,192},{64,160},{96,128},{128,96},{160,64},{192,32},{224... | collective-permute-start | bytes 737288 | tf_op jit(solution)/shard_map/ppermute | solution.py:261
  100.6 1.5 %collective-permute-start.16 = (bf16[240,512]{1,0:T(8,128)(2,1)S(1)}, bf16[240,512]{1,0:T(8,128)(2,1)S(1)}, u32[]{:S(2)}, u32[]{:S(2)}) collective-permute-start(bf16[240,512]{1,0:T(8,128)(2,1)S(1)} %bitcast.68), channel_id=1, source_target_pairs={{0,160},{32,128},{64,224},{96,192},{128,32},{160,0},{192,96},{224,... | collective-permute-start | bytes 737288 | tf_op jit(solution)/shard_map/ppermute | solution.py:261
  102.1 3.8 %update.6 = (bf16[5,48,512]{2,1,0:T(8,128)(2,1)S(1)}, bf16[5,48,512]{2,1,0:T(8,128)(2,1)S(1)}) custom-call(s32[8]{0:T(128)S(1)} %iota_xor_fusion.group_ref, f32[4,1600,128]{2,1,0:T(8,128)S(1)} %tip.1.weights_ref, bf16[4,40,48,128]{3,2,1,0:T(8,128)(2,1)S(1)} %copy-done.5, f32[4,48,128]{2,1,0:T(8,128)S(1)} %get-tuple-element.22.mean_ref), custom_call_target="tpu_custom_call" | custom-call | flops 6000000000 | bytes 8000000 | tf_op jit(solution)/shard_map/update/pallas_call | solution.py:246
  105.9 0.9 collective-permute-start.10
  106.8 2.6 %collective-permute-start.11 = (bf16[240,512]{1,0:T(8,128)(2,1)S(1)}, bf16[240,512]{1,0:T(8,128)(2,1)S(1)}, u32[]{:S(2)}, u32[]{:S(2)}) collective-permute-start(bf16[240,512]{1,0:T(8,128)(2,1)S(1)} %bitcast.62), channel_id=1, source_target_pairs={{0,64},{32,96},{64,0},{96,32},{128,192},{160,224},{192,128},{224,1... | collective-permute-start | bytes 737288 | tf_op jit(solution)/shard_map/ppermute | solution.py:261
  109.4 0.5 collective-permute-done.14.refs_0_
  109.9 0.7 collective-permute-start.12
  110.6 7.3 %collective-permute-done.15.refs_1_ = bf16[240,512]{1,0:T(8,128)(2,1)S(1)} collective-permute-done((bf16[240,512]{1,0:T(8,128)(2,1)S(1)}, bf16[240,512]{1,0:T(8,128)(2,1)S(1)}, u32[]{:S(2)}, u32[]{:S(2)}) %collective-permute-start.15) | collective-permute-done | bytes 245792 | tf_op jit(solution)/shard_map/ppermute | solution.py:261
  118.0 0.0 collective-permute-start.13
  118.0 0.0 collective-permute-done.16.refs_2_
  118.0 0.3 broadcast_in_dim.5.refs_4_
  118.3 4.9 %place.2.refs_5_ = bf16[240,4096]{1,0:T(8,128)(2,1)S(1)} custom-call(bf16[240,512]{1,0:T(8,128)(2,1)S(1)} %collective-permute-done.14.refs_0_, bf16[240,512]{1,0:T(8,128)(2,1)S(1)} %collective-permute-done.15.refs_1_, bf16[240,512]{1,0:T(8,128)(2,1)S(1)} %collective-permute-done.16.refs_2_, bf16[240,512]{1,0:T(8,128)(2,1)S(1)} %bitcast.77, ...), custom_call_target="tpu_custom_call" | custom-call | flops 4026531840 | bytes 3932160 | tf_op jit(solution)/shard_map/place/pallas_call | solution.py:79
  123.2 0.0 collective-permute-done.10.refs_0_
  123.3 0.1 collective-permute-done.11.refs_1_
  123.4 3.3 %collective-permute-done.12.refs_2_ = bf16[240,512]{1,0:T(8,128)(2,1)S(1)} collective-permute-done((bf16[240,512]{1,0:T(8,128)(2,1)S(1)}, bf16[240,512]{1,0:T(8,128)(2,1)S(1)}, u32[]{:S(2)}, u32[]{:S(2)}) %collective-permute-start.12) | collective-permute-done | bytes 245792 | tf_op jit(solution)/shard_map/ppermute | solution.py:261
  126.7 0.0 collective-permute-done.13.refs_3_
  126.7 0.3 broadcast_in_dim.4.refs_4_
  127.0 5.8 %place.3 = bf16[240,4096]{1,0:T(8,128)(2,1)} custom-call(bf16[240,512]{1,0:T(8,128)(2,1)S(1)} %collective-permute-done.10.refs_0_, bf16[240,512]{1,0:T(8,128)(2,1)S(1)} %collective-permute-done.11.refs_1_, bf16[240,512]{1,0:T(8,128)(2,1)S(1)} %collective-permute-done.12.refs_2_, bf16[240,512]{1,0:T(8,128)(2,1)S(1)} %collective-permute-done.13.refs_3_, ...), custom_call_target="tpu_custom_call" | custom-call | flops 4026531840 | bytes 3932160 | tf_op jit(solution)/shard_map/place/pallas_call | solution.py:79
  (19 shorter events, 0.2 us)
Async XLA Ops:
  0.0 1.1 copy-start.1
  1.1 3.5 %copy-start.2 = (s32[1,3,512]{2,0,1:T(1,128)S(1)}, s32[1,3,512]{2,0,1:T(1,128)}, u32[]{:S(2)}) copy-start(s32[1,3,512]{2,0,1:T(1,128)} %param.7) | copy-start | bytes 18436
  1.1 3.5 %copy-start.3 = (f32[1,3,512]{2,0,1:T(1,128)S(1)}, f32[1,3,512]{2,0,1:T(1,128)}, u32[]{:S(2)}) copy-start(f32[1,3,512]{2,0,1:T(1,128)} %param.8) | copy-start | bytes 18436
  1.4 5.1 %collective-permute-start = (bf16[16,1600]{1,0:T(8,128)(2,1)S(1)}, bf16[16,1600]{1,0:T(8,128)(2,1)S(1)}, u32[]{:S(2)}, u32[]{:S(2)}) collective-permute-start(bf16[16,1600]{1,0:T(8,128)(2,1)S(1)} %get-tuple-element.18), channel_id=1, source_target_pairs={{0,1},{1,2},{2,3},{3,4},{4,5},{5,6},{6,7},{7,8},{8,9},{9,10},{10,1... | collective-permute-start | bytes 153608 | tf_op jit(solution)/shard_map/ppermute | solution.py:280
  1.4 5.1 %collective-permute-start.1 = (bf16[16,1600]{1,0:T(8,128)(2,1)S(1)}, bf16[16,1600]{1,0:T(8,128)(2,1)S(1)}, u32[]{:S(2)}, u32[]{:S(2)}) collective-permute-start(bf16[16,1600]{1,0:T(8,128)(2,1)S(1)} %get-tuple-element.20), channel_id=1, source_target_pairs={{1,0},{2,1},{3,2},{4,3},{5,4},{6,5},{7,6},{8,7},{9,8},{10,9},{11,1... | collective-permute-start | bytes 153608 | tf_op jit(solution)/shard_map/ppermute | solution.py:281
  8.8 14.8 %copy-start.6 = (s32[32,8,16]{0,2,1:T(8,128)S(1)}, s32[32,8,16]{0,2,1:T(8,128)}, u32[]{:S(2)}) copy-start(s32[32,8,16]{0,2,1:T(8,128)} %param.6) | copy-start | bytes 49156
  8.8 75.2 %all-to-all-start = ((bf16[32,16,1600]{2,1,0:T(8,128)(2,1)}), bf16[32,16,1600]{2,1,0:T(8,128)(2,1)S(1)}, u32[]{:S(2)}, u32[]{:S(2)}) async-start(bf16[32,16,1600]{2,1,0:T(8,128)(2,1)} %bitcast.2), calls=%async_computation | async-start | bytes 3407872 | tf_op jit(solution)/shard_map/all_to_all | solution.py:288
  24.4 1.5 %copy-start = (bf16[5,48,4096]{2,1,0:T(8,128)(2,1)S(1)}, bf16[5,48,4096]{2,1,0:T(8,128)(2,1)}, u32[]{:S(2)}) copy-start(bf16[5,48,4096]{2,1,0:T(8,128)(2,1)} %param.5) | copy-start | bytes 5898244
  28.4 23.5 %collective-permute-start.5 = (bf16[2,240,512]{2,1,0:T(8,128)(2,1)S(1)}, bf16[2,240,512]{2,1,0:T(8,128)(2,1)S(1)}, u32[]{:S(2)}, u32[]{:S(2)}) collective-permute-start(bf16[2,240,512]{2,1,0:T(8,128)(2,1)S(1)} %pick.10), channel_id=1, source_target_pairs={{0,128},{32,160},{64,192},{96,224},{128,0},{160,32},{192,64},{224,... | collective-permute-start | bytes 1474568 | tf_op jit(solution)/shard_map/ppermute | solution.py:261
  29.8 38.7 %collective-permute-start.2 = (bf16[240,512]{1,0:T(8,128)(2,1)S(1)}, bf16[240,512]{1,0:T(8,128)(2,1)S(1)}, u32[]{:S(2)}, u32[]{:S(2)}) collective-permute-start(bf16[240,512]{1,0:T(8,128)(2,1)S(1)} %bitcast.69), channel_id=1, source_target_pairs={{0,32},{32,0},{64,96},{96,64},{128,160},{160,128},{192,224},{224,1... | collective-permute-start | bytes 737288 | tf_op jit(solution)/shard_map/ppermute | solution.py:261
  33.2 33.7 %collective-permute-start.7 = (bf16[2,240,512]{2,1,0:T(8,128)(2,1)S(1)}, bf16[2,240,512]{2,1,0:T(8,128)(2,1)S(1)}, u32[]{:S(2)}, u32[]{:S(2)}) collective-permute-start(bf16[2,240,512]{2,1,0:T(8,128)(2,1)S(1)} %pick.11), channel_id=1, source_target_pairs={{0,128},{32,160},{64,192},{96,224},{128,0},{160,32},{192,64},{224,... | collective-permute-start | bytes 1474568 | tf_op jit(solution)/shard_map/ppermute | solution.py:261
  36.5 35.3 %collective-permute-start.3 = (bf16[240,512]{1,0:T(8,128)(2,1)S(1)}, bf16[240,512]{1,0:T(8,128)(2,1)S(1)}, u32[]{:S(2)}, u32[]{:S(2)}) collective-permute-start(bf16[240,512]{1,0:T(8,128)(2,1)S(1)} %bitcast.65), channel_id=1, source_target_pairs={{0,64},{32,96},{64,0},{96,32},{128,192},{160,224},{192,128},{224,1... | collective-permute-start | bytes 737288 | tf_op jit(solution)/shard_map/ppermute | solution.py:261
  38.9 32.9 %collective-permute-start.4 = (bf16[240,512]{1,0:T(8,128)(2,1)S(1)}, bf16[240,512]{1,0:T(8,128)(2,1)S(1)}, u32[]{:S(2)}, u32[]{:S(2)}) collective-permute-start(bf16[240,512]{1,0:T(8,128)(2,1)S(1)} %bitcast.66), channel_id=1, source_target_pairs={{0,96},{32,64},{64,32},{96,0},{128,224},{160,192},{192,160},{224,1... | collective-permute-start | bytes 737288 | tf_op jit(solution)/shard_map/ppermute | solution.py:261
  51.9 19.9 %collective-permute-start.6 = (bf16[240,512]{1,0:T(8,128)(2,1)S(1)}, bf16[240,512]{1,0:T(8,128)(2,1)S(1)}, u32[]{:S(2)}, u32[]{:S(2)}) collective-permute-start(bf16[240,512]{1,0:T(8,128)(2,1)S(1)} %get-tuple-element.33), channel_id=1, source_target_pairs={{0,32},{32,0},{64,96},{96,64},{128,160},{160,128},{192,224},{224,1... | collective-permute-start | bytes 737288 | tf_op jit(solution)/shard_map/ppermute | solution.py:261
  66.9 9.5 %collective-permute-start.8 = (bf16[240,512]{1,0:T(8,128)(2,1)S(1)}, bf16[240,512]{1,0:T(8,128)(2,1)S(1)}, u32[]{:S(2)}, u32[]{:S(2)}) collective-permute-start(bf16[240,512]{1,0:T(8,128)(2,1)S(1)} %get-tuple-element.32), channel_id=1, source_target_pairs={{0,64},{32,96},{64,0},{96,32},{128,192},{160,224},{192,128},{224,1... | collective-permute-start | bytes 737288 | tf_op jit(solution)/shard_map/ppermute | solution.py:261
  68.4 13.2 %collective-permute-start.9 = (bf16[240,512]{1,0:T(8,128)(2,1)S(1)}, bf16[240,512]{1,0:T(8,128)(2,1)S(1)}, u32[]{:S(2)}, u32[]{:S(2)}) collective-permute-start(bf16[240,512]{1,0:T(8,128)(2,1)S(1)} %get-tuple-element.31), channel_id=1, source_target_pairs={{0,96},{32,64},{64,32},{96,0},{128,224},{160,192},{192,160},{224,1... | collective-permute-start | bytes 737288 | tf_op jit(solution)/shard_map/ppermute | solution.py:261
  82.8 1.3 copy-start.4
  84.0 1.5 %copy-start.5 = (bf16[4,40,48,128]{3,2,1,0:T(8,128)(2,1)S(1)}, bf16[4,40,48,128]{3,2,1,0:T(8,128)(2,1)}, u32[]{:S(2)}) copy-start(bf16[4,40,48,128]{3,2,1,0:T(8,128)(2,1)} %copy-done.4) | copy-start | bytes 5898244
  97.0 12.9 %collective-permute-start.14 = (bf16[240,512]{1,0:T(8,128)(2,1)S(1)}, bf16[240,512]{1,0:T(8,128)(2,1)S(1)}, u32[]{:S(2)}, u32[]{:S(2)}) collective-permute-start(bf16[240,512]{1,0:T(8,128)(2,1)S(1)} %bitcast.73), channel_id=1, source_target_pairs={{0,192},{32,224},{64,128},{96,160},{128,64},{160,96},{192,0},{224,... | collective-permute-start | bytes 737288 | tf_op jit(solution)/shard_map/ppermute | solution.py:261
  99.1 18.9 %collective-permute-start.15 = (bf16[240,512]{1,0:T(8,128)(2,1)S(1)}, bf16[240,512]{1,0:T(8,128)(2,1)S(1)}, u32[]{:S(2)}, u32[]{:S(2)}) collective-permute-start(bf16[240,512]{1,0:T(8,128)(2,1)S(1)} %bitcast.72), channel_id=1, source_target_pairs={{0,224},{32,192},{64,160},{96,128},{128,96},{160,64},{192,32},{224... | collective-permute-start | bytes 737288 | tf_op jit(solution)/shard_map/ppermute | solution.py:261
  100.6 17.4 %collective-permute-start.16 = (bf16[240,512]{1,0:T(8,128)(2,1)S(1)}, bf16[240,512]{1,0:T(8,128)(2,1)S(1)}, u32[]{:S(2)}, u32[]{:S(2)}) collective-permute-start(bf16[240,512]{1,0:T(8,128)(2,1)S(1)} %bitcast.68), channel_id=1, source_target_pairs={{0,160},{32,128},{64,224},{96,192},{128,32},{160,0},{192,96},{224,... | collective-permute-start | bytes 737288 | tf_op jit(solution)/shard_map/ppermute | solution.py:261
  105.9 17.4 %collective-permute-start.10 = (bf16[240,512]{1,0:T(8,128)(2,1)S(1)}, bf16[240,512]{1,0:T(8,128)(2,1)S(1)}, u32[]{:S(2)}, u32[]{:S(2)}) collective-permute-start(bf16[240,512]{1,0:T(8,128)(2,1)S(1)} %bitcast.63), channel_id=1, source_target_pairs={{0,128},{32,160},{64,192},{96,224},{128,0},{160,32},{192,64},{224,... | collective-permute-start | bytes 737288 | tf_op jit(solution)/shard_map/ppermute | solution.py:261
  106.8 16.6 %collective-permute-start.11 = (bf16[240,512]{1,0:T(8,128)(2,1)S(1)}, bf16[240,512]{1,0:T(8,128)(2,1)S(1)}, u32[]{:S(2)}, u32[]{:S(2)}) collective-permute-start(bf16[240,512]{1,0:T(8,128)(2,1)S(1)} %bitcast.62), channel_id=1, source_target_pairs={{0,64},{32,96},{64,0},{96,32},{128,192},{160,224},{192,128},{224,1... | collective-permute-start | bytes 737288 | tf_op jit(solution)/shard_map/ppermute | solution.py:261
  109.9 16.8 %collective-permute-start.12 = (bf16[240,512]{1,0:T(8,128)(2,1)S(1)}, bf16[240,512]{1,0:T(8,128)(2,1)S(1)}, u32[]{:S(2)}, u32[]{:S(2)}) collective-permute-start(bf16[240,512]{1,0:T(8,128)(2,1)S(1)} %bitcast.61), channel_id=1, source_target_pairs={{0,96},{32,64},{64,32},{96,0},{128,224},{160,192},{192,160},{224,1... | collective-permute-start | bytes 737288 | tf_op jit(solution)/shard_map/ppermute | solution.py:261
  118.0 8.7 %collective-permute-start.13 = (bf16[240,512]{1,0:T(8,128)(2,1)S(1)}, bf16[240,512]{1,0:T(8,128)(2,1)S(1)}, u32[]{:S(2)}, u32[]{:S(2)}) collective-permute-start(bf16[240,512]{1,0:T(8,128)(2,1)S(1)} %bitcast.67), channel_id=1, source_target_pairs={{0,32},{32,0},{64,96},{96,64},{128,160},{160,128},{192,224},{224,1... | collective-permute-start | bytes 737288 | tf_op jit(solution)/shard_map/ppermute | solution.py:261
